TPU v7x, 32 devices: a whole 2x2x4 slice. The times are simulated.
32 devices in a mesh: pop: 8 (over z, x), mp: 4 (over y, core).
Axes of the slice: x: 2, y: 2, z: 4, core: 2. Of those that a mesh axis runs over, the one named last changes fastest.
Arguments:
- tokens: bfloat16 [256, 3584], replicated, may hold values from -60 to 60
- target: bfloat16 [256, 3584], P(None, 'mp'), may hold values from -6 to 6
- w_query: bfloat16 [3584, 3584], P('pop', 'mp'), may hold values from -0.09375 to 0.09375
- w_key: bfloat16 [3584, 512], P(None, 'mp'), may hold values from -0.09375 to 0.09375
- w_value: bfloat16 [3584, 512], P(None, 'mp'), may hold values from -0.09375 to 0.09375
- w_out: bfloat16 [3584, 3584], P('mp', 'pop'), may hold values from -0.09375 to 0.09375
- query_left_factors: bfloat16 [8, 3584, 4], P('pop'), may hold values from -0.09375 to 0.09375
- query_right_factors: bfloat16 [8, 4, 3584], P('pop', None, 'mp'), may hold values from -6 to 6
- o_left: bfloat16 [8, 3584, 4], P('pop', 'mp'), may hold values from -0.09375 to 0.09375
- o_right: bfloat16 [8, 4, 3584], P('pop'), may hold values from -6 to 6
- member_ids: int32 [8], P('pop'), may hold values from 0 to 7, each once
Outputs:
- grad_query: float32 [3584, 3584], P('pop', 'mp')
- grad_out: float32 [3584, 3584], P('mp', 'pop')
- fitness: float32 [8], P('pop')
Inputs may be any that keep to these rules, and one draw needn't show every extreme that they name: `member_ids`: every number from 0 to 7 appears once.
All inputs are finite; a program needn't handle non-finite values.
Results may differ from a plain program's by a relative error of at most 0.005.
Values may be sent and summed in bfloat16 or wider, within the bound.
A program may use at most 64 MiB of HBM per device.

v0:
```python
import functools
import math

import jax
import jax.numpy as jnp
import numpy as np
from jax import lax
from jax.experimental import pallas as pl
from jax.experimental.pallas import tpu as pltpu
from jax.sharding import PartitionSpec as P

HEAD_DIM = 128
RANK = 4
PACK = 8
LINK = jnp.bfloat16

noise_scale = 0.5
rope_base = 1000000.0
spread_floor = 0.001
MESH = pl.DeviceIdType.MESH
f32 = jnp.float32
bf16 = jnp.bfloat16


def rope_tables(count, head_size):
    index = np.arange(head_size // 2, dtype=np.float64)
    freq = np.exp(-math.log(rope_base) * 2.0 * index / head_size)
    angle = np.arange(count, dtype=np.float64)[:, None] * freq[None, :]
    cosine, sine = np.cos(angle), np.sin(angle)
    return (
        np.concatenate([cosine, cosine], 1).astype(np.float32),
        np.concatenate([-sine, sine], 1).astype(np.float32),
    )


def dot(a, b, dims=((1,), (0,))):
    return lax.dot_general(a, b, (dims, ((), ())), preferred_element_type=f32)


def split3(x):
    hi = x.astype(bf16)
    rest = x - hi.astype(f32)
    mid = rest.astype(bf16)
    low = (rest - mid.astype(f32)).astype(bf16)
    return hi, mid, low


def forward_kernel(
    n_pop, n_mp, width,
    tok_hbm, wq_hbm, wk_hbm, wv_hbm, wo_hbm, tgt_hbm, ql_ref, qr_ref, ol_ref, or_ref, id_ref,
    cos_ref, sin_ref,
    pack_a_out, pack_b_out, stat_out,
    tok_ref, wq_ref, wk_ref, wv_ref, wo_ref, tgt_ref,
    part_a, part_b, parts_a, parts_b, mine_l, packs_l, mine_q, packs_q, mine_o, packs_o,
    mine_b, packs_b, ring_a, ring_b,
    terms, terms_in, tgt_own, target, errs, load_sem,
    pop_send, pop_recv,
    ring_send, ring_recv, term_send, term_recv, tgt_send, tgt_recv, err_send, err_recv,
):
    me = lax.axis_index("pop")
    mc = lax.axis_index("mp")
    n_dev = n_pop * n_mp
    tok, feats = tok_ref.shape[0], wq_ref.shape[1]
    cut = ring_a.shape[2]
    own_tok = tok // n_pop
    rows = n_pop * own_tok
    per_mp = rows // n_mp
    heads = feats // HEAD_DIM
    cols = wo_ref.shape[0]
    members = n_pop // n_mp
    odd = lax.rem(me, 2) == 1

    loads = [
        pltpu.make_async_copy(src, dst, load_sem.at[i])
        for i, (src, dst) in enumerate((
            (tok_hbm, tok_ref), (wq_hbm, wq_ref), (wk_hbm, wk_ref), (wv_hbm, wv_ref),
            (tgt_hbm, tgt_ref), (wo_hbm, wo_ref),
        ))
    ]
    for load in loads:
        load.start()

    barrier = pltpu.get_barrier_semaphore()

    def greet(i, carry):
        other = lax.rem(mc * n_pop + me + i, n_dev)
        pl.semaphore_signal(
            barrier, inc=1,
            device_id={"pop": lax.rem(other, n_pop), "mp": other // n_pop},
            device_id_type=MESH,
        )
        return carry

    lax.fori_loop(1, n_dev, greet, 0)

    sign = 1 - 2 * lax.rem(id_ref[0], 2)
    factor = noise_scale * sign.astype(f32)
    loads[0].wait()
    loads[1].wait()
    window = tok_ref[:, pl.ds(pl.multiple_of(me // 2 * 2 * cols, 128), 2 * cols)]
    wq = wq_ref[...]
    first, second = window[:, :cols], window[:, cols:]
    base = dot(jnp.where(odd, second, first), wq)
    part_a[...] = base[:, :cut].reshape(part_a.shape).astype(LINK)
    part_b[...] = base[:, cut:].reshape(part_b.shape).astype(LINK)
    mine_q[...] = (qr_ref[...].astype(f32) * factor).astype(bf16)

    pl.semaphore_wait(barrier, n_dev - 1)

    def to_pop(i, kind):
        other = lax.rem(me + i, n_pop)
        src, dst = (
            (part_a.at[other], parts_a),
            (mine_q, packs_q),
            (mine_l.at[other], packs_l),
            (part_b.at[other], parts_b),
            (mine_o, packs_o),
            (mine_b.at[other], packs_b),
        )[kind]
        return pltpu.make_async_remote_copy(
            src_ref=src, dst_ref=dst.at[me], send_sem=pop_send.at[kind, i],
            recv_sem=pop_recv.at[kind, i], device_id={"pop": other}, device_id_type=MESH,
        )

    def to_all(kind):
        for i in range(1, n_pop):
            to_pop(i, kind).start()

    def from_all(kind):
        for i in range(1, n_pop):
            to_pop(i, kind).wait_recv()

    to_all(0)
    to_all(1)
    ql = ql_ref[...]
    low = dot(ql, tok_ref[...], ((1,), (1,))).astype(bf16).astype(f32)
    for q in range(n_pop):
        mine_l[q] = jnp.concatenate(
            [low[:, q * own_tok:(q + 1) * own_tok], jnp.zeros((RANK, 128 - own_tok), f32)], axis=1
        ).astype(bf16)
    to_all(2)
    to_all(3)
    mine_o[...] = ol_ref[...]
    both = jnp.concatenate([ql.astype(f32), or_ref[...].astype(f32) * factor], axis=0)
    for q in range(n_pop):
        mine_b[q] = both[:, q * cols:(q + 1) * cols].astype(bf16)
    to_all(4)
    to_all(5)
    for mine, packs in ((part_a, parts_a), (part_b, parts_b), (mine_l, packs_l), (mine_b, packs_b)):
        packs[me] = mine[me]
    packs_q[me] = mine_q[...]
    packs_o[me] = mine_o[...]

    owner = me // (n_pop // n_mp)

    def target_copy(i):
        return pltpu.make_async_remote_copy(
            src_ref=tgt_own, dst_ref=target, send_sem=tgt_send.at[i], recv_sem=tgt_recv,
            device_id={"mp": lax.rem(mc + i, n_mp)}, device_id_type=MESH,
        )

    loads[4].wait()

    @pl.when(mc == owner)
    def _():
        tgt_own[...] = jnp.where(odd, tgt_ref[:, cols:], tgt_ref[:, :cols])
        for i in range(1, n_mp):
            target_copy(i).start()
        target[...] = tgt_own[...]

    loads[2].wait()
    loads[3].wait()
    cosine, sine = cos_ref[...], sin_ref[...]
    key = dot(tok_ref[...], wk_ref[...])
    key = (key * cosine + pltpu.roll(key, HEAD_DIM // 2, 1) * sine).astype(bf16)
    value = dot(tok_ref[...], wv_ref[...]).astype(bf16)

    start = pl.multiple_of(me * own_tok, own_tok)
    cos_own = jnp.tile(cos_ref[pl.ds(start, own_tok), :], (n_pop, 1))
    sin_own = jnp.tile(sin_ref[pl.ds(start, own_tok), :], (n_pop, 1))
    token_of = start + lax.rem(lax.broadcasted_iota(jnp.int32, (rows, tok), 0), own_tok)
    causal = token_of >= lax.broadcasted_iota(jnp.int32, (rows, tok), 1)
    scale = HEAD_DIM ** (-0.5)

    for kind in range(3):
        from_all(kind)

    def pop_at(r):
        r = lax.rem(r + 2 * n_pop, n_pop)
        return jnp.where(r < n_pop // 2, 2 * r, 2 * (n_pop - 1 - r) + 1)

    my_r = jnp.where(odd, n_pop - 1 - me // 2, me // 2)
    right, left = pop_at(my_r + 1), pop_at(my_r - 1)

    depth = n_pop // 2
    rings = (ring_a, ring_b)

    def hop(direction, step, g):
        at = pop_at(my_r - step if direction == 0 else my_r + step)
        return pltpu.make_async_remote_copy(
            src_ref=rings[g].at[at], dst_ref=rings[g].at[at],
            send_sem=ring_send.at[direction, step, g], recv_sem=ring_recv.at[direction, step, g],
            device_id={"pop": right if direction == 0 else left}, device_id_type=MESH,
        )

    def hops(direction, step, g):
        return step < depth - 1 or (step == depth - 1 and g == direction)

    def stacked(parts, *more):
        return jnp.concatenate(
            [p[i].astype(f32) for i in range(n_pop) for p in (parts,) + more], axis=0
        ).astype(bf16)

    pack_q = stacked(packs_q)
    ranks = n_pop * RANK
    eye = (
        lax.broadcasted_iota(jnp.int32, (ranks, ranks), 0)
        == lax.broadcasted_iota(jnp.int32, (ranks, ranks), 1)
    ).astype(bf16)
    low_rows = dot(stacked(packs_l), eye, ((0,), (0,)))[:own_tok]
    low_rows = jnp.tile(low_rows, (n_pop, 1))
    of_rank = lax.broadcasted_iota(jnp.int32, low_rows.shape, 1) // RANK
    of_row = lax.broadcasted_iota(jnp.int32, low_rows.shape, 0) // own_tok
    low_rows = jnp.where(of_rank == of_row, low_rows, 0.0).astype(bf16)
    group = ring_a.shape[2] // HEAD_DIM
    for h in range(heads):
        lanes = slice(h * HEAD_DIM, (h + 1) * HEAD_DIM)
        g = 0 if h < group else 1
        at = h - g * group
        here = slice(at * HEAD_DIM, (at + 1) * HEAD_DIM)
        if h == group:
            from_all(3)
        parts = (parts_a, parts_b)[g]
        total = parts[0, :, here].astype(f32)
        for i in range(1, n_pop):
            total = total + parts[i, :, here].astype(f32)
        q = jnp.tile(total, (n_pop, 1)) + dot(low_rows, pack_q[:, lanes])
        q = (q * cos_own + pltpu.roll(q, HEAD_DIM // 2, 1) * sin_own).astype(bf16)
        s = dot(q, key, ((1,), (1,))) * scale
        s = jnp.where(causal, s, -1e30)
        e = jnp.exp(s - jnp.max(s, axis=1, keepdims=True))
        prob = (e / jnp.sum(e, axis=1, keepdims=True)).astype(bf16)
        mixed = dot(prob, value).astype(bf16)
        rings[g][me, :, here] = mixed
        if h in (group - 1, heads - 1):
            for direction in range(2):
                hop(direction, 0, g).start()

    from_all(4)
    from_all(5)
    pack_a = stacked(packs_q, packs_o)
    pack_b = stacked(packs_b)
    pack_a_out[...] = pack_a
    pack_b_out[...] = pack_b
    loads[5].wait()

    def term_copy(at, block):
        return pltpu.make_async_remote_copy(
            src_ref=terms.at[at, block], dst_ref=terms_in.at[mc, at],
            send_sem=term_send.at[at, block], recv_sem=term_recv.at[mc, at],
            device_id={"mp": block}, device_id_type=MESH,
        )

    low_shape = (rows, n_pop * PACK)
    member_of = lax.broadcasted_iota(jnp.int32, low_shape, 0) // own_tok
    place = lax.broadcasted_iota(jnp.int32, low_shape, 1)
    keep = (place // PACK == member_of) & (lax.rem(place, PACK) >= RANK)

    def project(at):
        xa, xb = ring_a[at], ring_b[at]
        nt = ((1,), (1,))
        low = dot(xa, pack_a[:, :cut], nt) + dot(xb, pack_a[:, cut:], nt)
        low = jnp.where(keep, low, 0.0)
        y = dot(xa, wo_ref[:, :cut], nt) + dot(xb, wo_ref[:, cut:], nt)
        for piece in split3(low):
            y = y + dot(piece, pack_b)
        y = y.astype(bf16)
        for block in range(n_mp):
            terms[at, block] = y[block * per_mp:(block + 1) * per_mp]

            @pl.when(mc != block)
            def _():
                term_copy(at, block).start()

            @pl.when(mc == block)
            def _():
                terms_in[block, at] = terms[at, block]

    def squares(at, totals):
        for i in range(1, n_mp):
            source = lax.rem(mc + i, n_mp)
            pltpu.make_async_remote_copy(
                src_ref=terms.at[at, 0], dst_ref=terms_in.at[source, at],
                send_sem=term_send.at[at, 0], recv_sem=term_recv.at[source, at],
                device_id={"mp": source}, device_id_type=MESH,
            ).wait_recv()
        goal = target[pl.ds(pl.multiple_of(at * own_tok, own_tok), own_tok), :].astype(f32)
        result = []
        for k in range(members):
            span = slice(k * own_tok, (k + 1) * own_tok)
            out = terms_in[0, at, span].astype(f32)
            for c in range(1, n_mp):
                out = out + terms_in[c, at, span].astype(f32)
            diff = out - goal
            result.append(totals[k] + jnp.sum(diff * diff, axis=0, keepdims=True))
        return result

    project(me)

    @pl.when(mc != owner)
    def _():
        target_copy(1).wait_recv()

    totals = [jnp.zeros((1, cols), f32)] * members
    done = [me]
    for step in range(depth):
        for g in range(2):
            for direction in range(2):
                if hops(direction, step, g):
                    hop(direction, step, g).wait_recv()
                    if hops(direction, step + 1, g):
                        hop(direction, step + 1, g).start()
        landed = [pop_at(my_r - 1 - step)]
        if step < depth - 1:
            landed.append(pop_at(my_r + 1 + step))
        for at in landed:
            project(at)
        for at in done:
            totals = squares(at, totals)
        done = landed
    for at in done:
        totals = squares(at, totals)

    lane_row = lax.broadcasted_iota(jnp.int32, (1, 128), 1)
    mine = jnp.zeros((1, 128), f32)
    for k in range(members):
        value_k = jnp.sum(totals[k], axis=1, keepdims=True)
        mine = mine + jnp.where(lane_row == mc * members + k, value_k, 0.0)

    my_id = mc * n_pop + me
    errs[my_id] = mine

    def err_copy(i):
        other = lax.rem(my_id + i, n_dev)
        return pltpu.make_async_remote_copy(
            src_ref=errs.at[my_id], dst_ref=errs.at[my_id],
            send_sem=err_send.at[i], recv_sem=err_recv.at[i],
            device_id={"pop": lax.rem(other, n_pop), "mp": other // n_pop}, device_id_type=MESH,
        )

    def err_start(i, carry):
        err_copy(i).start()
        return carry

    def err_wait(i, carry):
        err_copy(i).wait_recv()
        return carry

    lax.fori_loop(1, n_dev, err_start, 0)
    for kind in range(6):
        for i in range(1, n_pop):
            to_pop(i, kind).wait_send()
    for step in range(depth):
        for g in range(2):
            for direction in range(2):
                if hops(direction, step, g):
                    hop(direction, step, g).wait_send()
    for block in range(n_mp):
        @pl.when(mc != block)
        def _():
            for at in range(n_pop):
                term_copy(at, block).wait_send()

    @pl.when(mc == owner)
    def _():
        for i in range(1, n_mp):
            target_copy(i).wait_send()

    lax.fori_loop(1, n_dev, err_wait, 0)
    error = errs[0]
    for i in range(1, n_dev):
        error = error + errs[i]
    live = lane_row < n_pop
    fitness = -(error / (tok * width))
    mean = jnp.sum(jnp.where(live, fitness, 0.0), axis=1, keepdims=True) / n_pop
    dev = jnp.where(live, fitness - mean, 0.0)
    spread = jnp.sum(dev * dev, axis=1, keepdims=True) / n_pop
    weight = dev / jnp.sqrt(spread + spread_floor)
    stat_out[...] = jnp.concatenate(
        [fitness, weight, jnp.zeros((6, 128), f32)], axis=0
    )

    def err_drain(i, carry):
        err_copy(i).wait_send()
        return carry

    lax.fori_loop(1, n_dev, err_drain, 0)


def grad_kernel(a_ref, b_ref, stat_ref, gq_hbm, got_hbm, fit_ref, gq_ref, got_ref, sem):
    pack_a = a_ref[...]
    pack_b = b_ref[...].astype(f32)
    rows, cols = pack_b.shape
    row = lax.broadcasted_iota(jnp.int32, (rows, 128), 0)
    lane = lax.broadcasted_iota(jnp.int32, (rows, 128), 1)
    per_row = jnp.sum(jnp.where(lane == row // PACK, stat_ref[1:2, :], 0.0), axis=1, keepdims=True)
    per_row = per_row / (noise_scale * noise_scale)
    kind = lax.rem(lax.broadcasted_iota(jnp.int32, (rows, 1), 0), PACK)
    edges = (0, (cols // 2 + 127) // 128 * 128, cols)
    copies = []
    for out, target, weight in (
        (gq_ref, gq_hbm, jnp.where(kind < RANK, per_row, 0.0)),
        (got_ref, got_hbm, jnp.where(kind >= RANK, per_row, 0.0)),
    ):
        pieces = jnp.concatenate(split3(pack_b * weight), axis=0)
        right = jnp.concatenate([pack_a] * 3, axis=0)
        for low, high in zip(edges[:-1], edges[1:]):
            out[low:high, :] = dot(pieces[:, low:high], right, ((0,), (0,)))
            copy = pltpu.make_async_copy(
                out.at[low:high], target.at[low:high], sem.at[len(copies)]
            )
            copy.start()
            copies.append(copy)
    me = lax.axis_index("pop")
    fit_ref[0] = jnp.sum(jnp.where(lane[:1] == me, stat_ref[0:1, :], 0.0))
    for copy in copies:
        copy.wait()


def per_device_fast(
    n_pop, n_mp,
    tokens, target, w_query, w_key, w_value, w_out,
    query_left_factors, query_right_factors, o_left, o_right, member_ids,
):
    tok, width = tokens.shape
    feats = w_query.shape[1]
    cols = w_out.shape[1]
    own_tok = tok // n_pop
    rows = n_pop * own_tok
    cosine, sine = rope_tables(tok, HEAD_DIM)
    vmem = pl.BlockSpec(memory_space=pltpu.VMEM)
    hbm = pl.BlockSpec(memory_space=pltpu.HBM)
    smem = pl.BlockSpec(memory_space=pltpu.SMEM)
    dma = pltpu.SemaphoreType.DMA
    depth = n_pop // 2
    n_dev = n_pop * n_mp
    cut = (feats // HEAD_DIM + 1) // 2 * HEAD_DIM
    like = lambda x: pltpu.VMEM(x.shape, x.dtype)
    wot = w_out.T
    pack_a, pack_b, stat = pl.pallas_call(
        functools.partial(forward_kernel, n_pop, n_mp, width),
        name="forward",
        out_shape=(
            jax.ShapeDtypeStruct((n_pop * PACK, feats), bf16),
            jax.ShapeDtypeStruct((n_pop * PACK, cols), bf16),
            jax.ShapeDtypeStruct((8, 128), f32),
        ),
        in_specs=[hbm] * 6 + [vmem] * 4 + [smem] + [vmem] * 2,
        out_specs=(vmem, vmem, vmem),
        scratch_shapes=[
            like(tokens), like(w_query), like(w_key), like(w_value), like(wot), like(target),
            pltpu.VMEM((n_pop, own_tok, cut), LINK),
            pltpu.VMEM((n_pop, own_tok, feats - cut), LINK),
            pltpu.VMEM((n_pop, own_tok, cut), LINK),
            pltpu.VMEM((n_pop, own_tok, feats - cut), LINK),
            pltpu.VMEM((n_pop, RANK, 128), bf16),
            pltpu.VMEM((n_pop, RANK, 128), bf16),
            pltpu.VMEM((RANK, feats), bf16),
            pltpu.VMEM((n_pop, RANK, feats), bf16),
            pltpu.VMEM((RANK, feats), bf16),
            pltpu.VMEM((n_pop, RANK, feats), bf16),
            pltpu.VMEM((n_pop, PACK, cols), bf16),
            pltpu.VMEM((n_pop, PACK, cols), bf16),
            pltpu.VMEM((n_pop, rows, cut), bf16),
            pltpu.VMEM((n_pop, rows, feats - cut), bf16),
            pltpu.VMEM((n_pop, n_mp, rows // n_mp, cols), bf16),
            pltpu.VMEM((n_mp, n_pop, rows // n_mp, cols), bf16),
            pltpu.VMEM((tok, cols), bf16),
            pltpu.VMEM((tok, cols), bf16),
            pltpu.VMEM((n_dev, 1, 128), f32),
            dma((6,)),
            dma((6, n_pop)), dma((6, n_pop)),
            dma((2, depth, 2)), dma((2, depth, 2)),
            dma((n_pop, n_mp)), dma((n_mp, n_pop)),
            dma((n_mp,)), dma,
            dma((n_dev,)), dma((n_dev,)),
        ],
        compiler_params=pltpu.CompilerParams(
            collective_id=0, has_side_effects=True, vmem_limit_bytes=60 * 1024 * 1024
        ),
    )(tokens, w_query, w_key, w_value, wot, target,
      query_left_factors[0].T, query_right_factors[0], o_left[0].T, o_right[0], member_ids,
      jnp.asarray(cosine), jnp.asarray(sine))
    grad = jax.ShapeDtypeStruct((cols, feats), f32)
    grad_query, grad_out_t, fitness = pl.pallas_call(
        grad_kernel,
        name="grads",
        out_shape=(grad, grad, jax.ShapeDtypeStruct((1,), f32)),
        in_specs=[vmem, vmem, vmem],
        out_specs=(hbm, hbm, smem),
        scratch_shapes=[like(grad), like(grad), dma((4,))],
    )(pack_a, pack_b, stat)
    return grad_query, grad_out_t.T, fitness


def tables(count, head_size):
    position = jnp.arange(count, dtype=jnp.float32)
    index = jnp.arange(head_size // 2, dtype=jnp.float32)
    freq = jnp.exp(-math.log(rope_base) * 2.0 * index / head_size)
    angle = position[:, None] * freq[None, :]
    return (jnp.cos(angle)[:, None, :], jnp.sin(angle)[:, None, :])


def rotate(field, cosine_table, sine):
    half = field.shape[-1] // 2
    first = field[..., :half]
    second = field[..., half:]
    return jnp.concatenate(
        [first * cosine_table - second * sine, second * cosine_table + first * sine], axis=-1
    )


def per_device(
    tokens,
    target,
    w_query,
    w_key,
    w_value,
    w_out,
    query_left_factors,
    query_right_factors,
    o_left,
    o_right,
    member_ids,
):
    tok = tokens.shape[0]
    local_feats = w_query.shape[1]
    local_kv = w_key.shape[1] // HEAD_DIM
    group = group_of(w_query, w_key)
    local_heads = local_kv * group
    slots = query_left_factors.shape[0]
    scale = HEAD_DIM ** (-0.5)
    cosine_table, sine = tables(tok, HEAD_DIM)
    base = jnp.dot(
        tokens,
        lax.all_gather(w_query, "pop", axis=0, tiled=True),
        preferred_element_type=jnp.float32,
    )
    keys = rotate(
        jnp.dot(tokens, w_key, preferred_element_type=jnp.float32).reshape(tok, local_kv, HEAD_DIM),
        cosine_table,
        sine,
    ).astype(jnp.bfloat16)
    values = (
        jnp.dot(tokens, w_value, preferred_element_type=jnp.float32)
        .astype(jnp.bfloat16)
        .reshape(tok, local_kv, HEAD_DIM)
    )
    signs = (1 - 2 * (member_ids % 2)).astype(jnp.float32)
    factor = noise_scale * signs[:, None, None]
    lowrank_product = jnp.einsum(
        "td,mdr->mtr", tokens, query_left_factors, preferred_element_type=jnp.float32
    ).astype(jnp.bfloat16)
    query = base[None] + factor * jnp.einsum(
        "olj,ojv->olv", lowrank_product, query_right_factors, preferred_element_type=jnp.float32
    )
    query = rotate(
        query.reshape(slots, tok, local_heads, HEAD_DIM), cosine_table[None], sine[None]
    ).astype(jnp.bfloat16)
    query = query.reshape(slots, tok, local_kv, group, HEAD_DIM)
    scores = jnp.einsum("mtkgd,skd->mkgts", query, keys, preferred_element_type=jnp.float32) * scale
    causal = jnp.arange(tok)[:, None] >= jnp.arange(tok)[None, :]
    scores = jnp.where(causal, scores, -1e30)
    probs = jax.nn.softmax(scores, axis=-1).astype(jnp.bfloat16)
    mixed = (
        jnp.einsum("mkgts,skd->mtkgd", probs, values, preferred_element_type=jnp.float32)
        .astype(jnp.bfloat16)
        .reshape(slots, tok, local_feats)
    )
    low_out = jnp.einsum("mtf,mfr->mtr", mixed, o_left, preferred_element_type=jnp.float32)
    right_full = o_right.astype(jnp.float32)
    part = jnp.einsum(
        "mtf,fe->mte",
        mixed,
        lax.all_gather(w_out, "pop", axis=1, tiled=True),
        preferred_element_type=jnp.float32,
    )
    term = part + factor * jnp.einsum(
        "mtr,mre->mte", low_out, right_full, precision=lax.Precision.HIGHEST
    )
    output = lax.psum_scatter(
        term.astype(jnp.bfloat16), "mp", scatter_dimension=2, tiled=True
    ).astype(jnp.float32)
    diff = output - target.astype(jnp.float32)[None]
    errors = lax.psum(jnp.sum(diff * diff, axis=(1, 2)), "mp")
    fitness = -(errors / (tok * tokens.shape[1]))
    count = slots * lax.axis_size("pop")
    mean = lax.psum(jnp.sum(fitness), "pop") / count
    spread = lax.psum(jnp.sum((fitness - mean) * (fitness - mean)), "pop") / count
    weight = signs * (fitness - mean) / jnp.sqrt(spread + spread_floor)
    every_weight = lax.all_gather(weight, "pop", axis=0, tiled=True)
    right_factors_gathered, left_all = (
        lax.all_gather(query_right_factors, "pop", axis=0, tiled=True),
        lax.all_gather(o_left, "pop", axis=0, tiled=True),
    )
    rows_q = lax.all_to_all(query_left_factors, "pop", split_axis=1, concat_axis=0, tiled=True)
    cols_o = lax.all_to_all(o_right, "pop", split_axis=2, concat_axis=0, tiled=True)
    whole_population = rows_q.shape[0]
    left_q = jnp.transpose(
        rows_q.astype(jnp.float32) * every_weight[:, None, None], (1, 0, 2)
    ).reshape(rows_q.shape[1], whole_population * RANK)
    right_q = right_factors_gathered.astype(jnp.float32).reshape(
        whole_population * RANK, local_feats
    )
    grad_query = jnp.dot(left_q, right_q, precision=lax.Precision.HIGHEST) / noise_scale
    output_left_factor = jnp.transpose(
        left_all.astype(jnp.float32) * every_weight[:, None, None], (1, 0, 2)
    ).reshape(local_feats, whole_population * RANK)
    right_o = cols_o.astype(jnp.float32).reshape(whole_population * RANK, cols_o.shape[2])
    grad_out = jnp.dot(output_left_factor, right_o, precision=lax.Precision.HIGHEST) / noise_scale
    return (grad_query, grad_out, fitness)


def group_of(w_query, w_key):
    return w_query.shape[1] // w_key.shape[1]


def pick(args, n_pop, n_mp):
    tok = args[0].shape[0]
    kernel = (
        args[6].shape[0] == n_pop
        and n_pop % n_mp == 0
        and n_pop % 2 == 0
        and n_pop * PACK <= 128
        and tok % (n_pop * 16) == 0
        and tok // n_pop < 128
        and args[2].shape[1] // n_mp == 2 * args[5].shape[1] // n_pop
        and args[2].shape[0] == args[5].shape[1]
        and args[3].shape[1] == n_mp * HEAD_DIM
    )
    return functools.partial(per_device_fast, n_pop, n_mp) if kernel else per_device


def solution(mesh):
    placed = (
        P(),
        P(None, "mp"),
        P("pop", "mp"),
        P(None, "mp"),
        P(None, "mp"),
        P("mp", "pop"),
        P("pop", None, None),
        P("pop", None, "mp"),
        P("pop", "mp", None),
        P("pop", None, None),
        P("pop"),
    )
    n_pop, n_mp = mesh.shape["pop"], mesh.shape["mp"]

    def whole(*args):
        return jax.shard_map(
            pick(args, n_pop, n_mp),
            mesh=mesh,
            in_specs=placed,
            out_specs=(P("pop", "mp"), P("mp", "pop"), P("pop")),
            check_vma=False,
        )(*args)

    return whole
```

profile of v0, /device:TPU:0, one launch (start us, length us, event | category | flops | bytes accessed | tf_op | source)
XLA Modules:
  0.0 76.1 jit_solution(7999476859627990513)
XLA Ops:
  1.3 71.2 %forward.1 = (bf16[64,896]{1,0:T(8,128)(2,1)}, bf16[64,448]{1,0:T(8,128)(2,1)}, f32[8,128]{1,0:T(8,128)}) custom-call(bf16[256,3584]{1,0:T(8,128)(2,1)} %tok_hbm.1, bf16[448,896]{1,0:T(8,128)(2,1)} %wq_hbm.1, bf16[3584,128]{1,0:T(8,128)(2,1)} %wk_hbm.1, bf16[3584,128]{1,0:T(8,128)(2,1)} %wv_hbm.1, bf16[448,896]{1,0:T(8,128)(2,1)} %bitcast.10, ...), custom_call_target="tpu_custom_call" | custom-call | tf_op jit(solution)/shard_map/forward/pallas_call | solution.py:450
  72.5 3.6 %grads.1 = (f32[448,896]{1,0:T(8,128)}, f32[448,896]{1,0:T(8,128)}, f32[1]{0:T(128)}) custom-call(bf16[64,896]{1,0:T(8,128)(2,1)} %get-tuple-element.9.a_ref, bf16[64,448]{1,0:T(8,128)(2,1)} %get-tuple-element.10.b_ref, f32[8,128]{1,0:T(8,128)} %get-tuple-element.11.stat_ref), custom_call_target="tpu_custom_call" | custom-call | tf_op jit(solution)/shard_map/grads/pallas_call | solution.py:495
where the time goes:
time: 76.3 us; the launch traced here: 76.1 us
  Pallas kernels  74.8 us (98%)
  between operations  1.29 us (2%)
    pallas_call x1, Pallas kernels, per_device_fast(): pl.pallas_call(functools.partial(forward_kernel, n_pop, n_mp, width), nam...  71.2 us
    pallas_call x1, Pallas kernels, per_device_fast(): pl.pallas_call(grad_kernel, name='grads', out_shape=(grad, grad, jax.Shap...  3.6 us

commit v1 on v0

--- a/solution.py
+++ b/solution.py
@@ -48,14 +48,15 @@
 def forward_kernel(
     n_pop, n_mp, width,
     tok_hbm, wq_hbm, wk_hbm, wv_hbm, wo_hbm, tgt_hbm, ql_ref, qr_ref, ol_ref, or_ref, id_ref,
-    cos_ref, sin_ref,
+    cos_ref, sin_ref, cos_rows, sin_rows,
     pack_a_out, pack_b_out, stat_out,
-    tok_ref, wq_ref, wk_ref, wv_ref, wo_ref, tgt_ref,
+    tok_ref, wq_ref, kv_ref, wo_ref, tgt_ref,
     part_a, part_b, parts_a, parts_b, mine_l, packs_l, mine_q, packs_q, mine_o, packs_o,
     mine_b, packs_b, ring_a, ring_b,
-    terms, terms_in, tgt_own, target, errs, load_sem,
+    keys, values, low_rows, goal, mixed, terms, near_in, far_out, far_in, own_sum, total, errs,
+    load_sem,
     pop_send, pop_recv,
-    ring_send, ring_recv, term_send, term_recv, tgt_send, tgt_recv, err_send, err_recv,
+    ring_send, ring_recv, near_send, near_recv, far_send, far_recv, err_send, err_recv,
 ):
     me = lax.axis_index("pop")
     mc = lax.axis_index("mp")
@@ -64,17 +65,18 @@
     cut = ring_a.shape[2]
     own_tok = tok // n_pop
     rows = n_pop * own_tok
-    per_mp = rows // n_mp
     heads = feats // HEAD_DIM
-    cols = wo_ref.shape[0]
-    members = n_pop // n_mp
+    cols = wq_ref.shape[0]
+    ranks = n_pop * RANK
+    quarter = cols // n_mp
     odd = lax.rem(me, 2) == 1
 
     loads = [
         pltpu.make_async_copy(src, dst, load_sem.at[i])
         for i, (src, dst) in enumerate((
-            (tok_hbm, tok_ref), (wq_hbm, wq_ref), (wk_hbm, wk_ref), (wv_hbm, wv_ref),
-            (tgt_hbm, tgt_ref), (wo_hbm, wo_ref),
+            (tok_hbm, tok_ref), (wq_hbm, wq_ref),
+            (wk_hbm, kv_ref.at[:, :HEAD_DIM]), (wv_hbm, kv_ref.at[:, HEAD_DIM:]),
+            (tgt_hbm, tgt_ref), (wo_hbm, wo_ref.at[:cols]),
         ))
     ]
     for load in loads:
@@ -112,7 +114,7 @@
         src, dst = (
             (part_a.at[other], parts_a),
             (mine_q, packs_q),
-            (mine_l.at[other], packs_l),
+            (mine_l, packs_l),
             (part_b.at[other], parts_b),
             (mine_o, packs_o),
             (mine_b.at[other], packs_b),
@@ -133,11 +135,7 @@
     to_all(0)
     to_all(1)
     ql = ql_ref[...]
-    low = dot(ql, tok_ref[...], ((1,), (1,))).astype(bf16).astype(f32)
-    for q in range(n_pop):
-        mine_l[q] = jnp.concatenate(
-            [low[:, q * own_tok:(q + 1) * own_tok], jnp.zeros((RANK, 128 - own_tok), f32)], axis=1
-        ).astype(bf16)
+    mine_l[...] = dot(ql, tok_ref[...], ((1,), (1,))).astype(bf16)
     to_all(2)
     to_all(3)
     mine_o[...] = ol_ref[...]
@@ -146,44 +144,50 @@
         mine_b[q] = both[:, q * cols:(q + 1) * cols].astype(bf16)
     to_all(4)
     to_all(5)
-    for mine, packs in ((part_a, parts_a), (part_b, parts_b), (mine_l, packs_l), (mine_b, packs_b)):
+    for mine, packs in ((part_a, parts_a), (part_b, parts_b), (mine_b, packs_b)):
         packs[me] = mine[me]
+    packs_l[me] = mine_l[...]
     packs_q[me] = mine_q[...]
     packs_o[me] = mine_o[...]
 
-    owner = me // (n_pop // n_mp)
-
-    def target_copy(i):
-        return pltpu.make_async_remote_copy(
-            src_ref=tgt_own, dst_ref=target, send_sem=tgt_send.at[i], recv_sem=tgt_recv,
-            device_id={"mp": lax.rem(mc + i, n_mp)}, device_id_type=MESH,
-        )
-
-    loads[4].wait()
-
-    @pl.when(mc == owner)
-    def _():
-        tgt_own[...] = jnp.where(odd, tgt_ref[:, cols:], tgt_ref[:, :cols])
-        for i in range(1, n_mp):
-            target_copy(i).start()
-        target[...] = tgt_own[...]
-
     loads[2].wait()
     loads[3].wait()
-    cosine, sine = cos_ref[...], sin_ref[...]
-    key = dot(tok_ref[...], wk_ref[...])
-    key = (key * cosine + pltpu.roll(key, HEAD_DIM // 2, 1) * sine).astype(bf16)
-    value = dot(tok_ref[...], wv_ref[...]).astype(bf16)
-
-    start = pl.multiple_of(me * own_tok, own_tok)
-    cos_own = jnp.tile(cos_ref[pl.ds(start, own_tok), :], (n_pop, 1))
-    sin_own = jnp.tile(sin_ref[pl.ds(start, own_tok), :], (n_pop, 1))
-    token_of = start + lax.rem(lax.broadcasted_iota(jnp.int32, (rows, tok), 0), own_tok)
-    causal = token_of >= lax.broadcasted_iota(jnp.int32, (rows, tok), 1)
-    scale = HEAD_DIM ** (-0.5)
-
-    for kind in range(3):
-        from_all(kind)
+    pair = dot(tok_ref[...], kv_ref[...])
+    key = pair[:, :HEAD_DIM]
+    key = (key * cos_ref[...] + pltpu.roll(key, HEAD_DIM // 2, 1) * sin_ref[...]).astype(bf16)
+    values[:HEAD_DIM] = pair[:, HEAD_DIM:].T.astype(bf16)
+    values[HEAD_DIM:] = jnp.ones((values.shape[0] - HEAD_DIM, tok), bf16)
+    spot = lax.broadcasted_iota(jnp.int32, (tok, HEAD_DIM), 0)
+    lane = lax.broadcasted_iota(jnp.int32, (tok, HEAD_DIM), 1)
+    for q in range(n_pop):
+        keys[q, :, :HEAD_DIM] = key
+        hidden = (spot > q * own_tok + lane) & (lane < own_tok)
+        keys[q, :, HEAD_DIM:] = jnp.where(hidden, -1e30, 0.0).astype(bf16)
+
+    loads[4].wait()
+    owner = me // (n_pop // n_mp)
+    tgt = jnp.where(odd, tgt_ref[:, cols:], tgt_ref[:, :cols])
+    goal[...] = jnp.where(mc == owner, -tgt, jnp.zeros_like(tgt))
+
+    row_tok = lax.rem(lax.broadcasted_iota(jnp.int32, (own_tok, rows), 1), own_tok)
+    pick_tok = (row_tok == lax.broadcasted_iota(jnp.int32, (own_tok, rows), 0)).astype(bf16)
+    row_member = lax.broadcasted_iota(jnp.int32, (ranks, rows), 1) // own_tok
+    same = row_member == lax.broadcasted_iota(jnp.int32, (ranks, rows), 0) // RANK
+
+    def stacked(parts, *more):
+        return jnp.concatenate(
+            [p[i].astype(f32) for i in range(n_pop) for p in (parts,) + more], axis=0
+        ).astype(bf16)
+
+    from_all(1)
+    from_all(2)
+    pack_q = stacked(packs_q)
+    low_all = stacked(packs_l)
+    spot = lax.broadcasted_iota(jnp.int32, (tok, rows), 0)
+    at_tok = lax.rem(lax.broadcasted_iota(jnp.int32, (tok, rows), 1), own_tok)
+    for q in range(n_pop):
+        sel = (spot == at_tok + q * own_tok).astype(bf16)
+        low_rows[q] = jnp.where(same, dot(low_all, sel), 0.0).astype(bf16)
 
     def pop_at(r):
         r = lax.rem(r + 2 * n_pop, n_pop)
@@ -206,136 +210,135 @@
     def hops(direction, step, g):
         return step < depth - 1 or (step == depth - 1 and g == direction)
 
-    def stacked(parts, *more):
-        return jnp.concatenate(
-            [p[i].astype(f32) for i in range(n_pop) for p in (parts,) + more], axis=0
-        ).astype(bf16)
-
-    pack_q = stacked(packs_q)
-    ranks = n_pop * RANK
-    eye = (
-        lax.broadcasted_iota(jnp.int32, (ranks, ranks), 0)
-        == lax.broadcasted_iota(jnp.int32, (ranks, ranks), 1)
-    ).astype(bf16)
-    low_rows = dot(stacked(packs_l), eye, ((0,), (0,)))[:own_tok]
-    low_rows = jnp.tile(low_rows, (n_pop, 1))
-    of_rank = lax.broadcasted_iota(jnp.int32, low_rows.shape, 1) // RANK
-    of_row = lax.broadcasted_iota(jnp.int32, low_rows.shape, 0) // own_tok
-    low_rows = jnp.where(of_rank == of_row, low_rows, 0.0).astype(bf16)
-    group = ring_a.shape[2] // HEAD_DIM
-    for h in range(heads):
-        lanes = slice(h * HEAD_DIM, (h + 1) * HEAD_DIM)
-        g = 0 if h < group else 1
-        at = h - g * group
-        here = slice(at * HEAD_DIM, (at + 1) * HEAD_DIM)
-        if h == group:
-            from_all(3)
-        parts = (parts_a, parts_b)[g]
-        total = parts[0, :, here].astype(f32)
+    for g, (kind, parts) in enumerate(((0, parts_a), (3, parts_b))):
+        from_all(kind)
+        sum_g = parts[0].astype(f32)
         for i in range(1, n_pop):
-            total = total + parts[i, :, here].astype(f32)
-        q = jnp.tile(total, (n_pop, 1)) + dot(low_rows, pack_q[:, lanes])
-        q = (q * cos_own + pltpu.roll(q, HEAD_DIM // 2, 1) * sin_own).astype(bf16)
-        s = dot(q, key, ((1,), (1,))) * scale
-        s = jnp.where(causal, s, -1e30)
-        e = jnp.exp(s - jnp.max(s, axis=1, keepdims=True))
-        prob = (e / jnp.sum(e, axis=1, keepdims=True)).astype(bf16)
-        mixed = dot(prob, value).astype(bf16)
-        rings[g][me, :, here] = mixed
-        if h in (group - 1, heads - 1):
-            for direction in range(2):
-                hop(direction, 0, g).start()
+            sum_g = sum_g + parts[i].astype(f32)
+        rings[g][me] = sum_g.astype(LINK)
+        for direction in range(2):
+            hop(direction, 0, g).start()
 
     from_all(4)
     from_all(5)
-    pack_a = stacked(packs_q, packs_o)
-    pack_b = stacked(packs_b)
-    pack_a_out[...] = pack_a
-    pack_b_out[...] = pack_b
+    pack_a_out[...] = stacked(packs_q, packs_o)
+    pack_b_out[...] = stacked(packs_b)
+    right_o = jnp.concatenate(
+        [packs_b[i, RANK:].astype(f32) for i in range(n_pop)], axis=0
+    ).astype(bf16)
     loads[5].wait()
-
-    def term_copy(at, block):
+    wo_ref[cols:] = stacked(packs_o)
+    total[...] = jnp.zeros_like(total)
+
+    scale = HEAD_DIM ** (-0.5) * math.log2(math.e)
+    half = HEAD_DIM // 2
+    filler = jnp.zeros((keys.shape[2] - HEAD_DIM - own_tok, rows), bf16)
+
+    def attend(at):
+        cosine = jnp.concatenate([cos_rows[at]] * (rows // 128), axis=1)
+        sine = jnp.concatenate([sin_rows[at]] * (rows // 128), axis=1)
+        mix = jnp.concatenate([pick_tok, low_rows[at]], axis=0)
+        for h in range(heads):
+            lanes = slice(h * HEAD_DIM, (h + 1) * HEAD_DIM)
+            g = 0 if (h + 1) * HEAD_DIM <= cut else 1
+            here = slice(h * HEAD_DIM - g * cut, (h + 1) * HEAD_DIM - g * cut)
+            left_q = jnp.concatenate([rings[g][at, :, here], pack_q[:, lanes]], axis=0)
+            q = dot(left_q, mix, ((0,), (0,)))
+            low, high = q[:half], q[half:]
+            q = jnp.concatenate(
+                [low * cosine - high * sine, high * cosine + low * sine], axis=0
+            ).astype(bf16)
+            s = dot(keys[at], jnp.concatenate([q, pick_tok, filler], axis=0))
+            e = jnp.exp2((s - jnp.max(s, axis=0, keepdims=True)) * scale).astype(bf16)
+            out = dot(values[...], e)
+            inverse = 1.0 / out[HEAD_DIM:HEAD_DIM + 1]
+            mixed[lanes] = (out[:HEAD_DIM] * inverse).astype(bf16)
+
+    def near_copy(at):
         return pltpu.make_async_remote_copy(
-            src_ref=terms.at[at, block], dst_ref=terms_in.at[mc, at],
-            send_sem=term_send.at[at, block], recv_sem=term_recv.at[mc, at],
-            device_id={"mp": block}, device_id_type=MESH,
+            src_ref=terms.at[at, 1 - lax.rem(mc, 2)], dst_ref=near_in.at[at],
+            send_sem=near_send.at[at], recv_sem=near_recv.at[at],
+            device_id={"mp": mc + 1 - 2 * lax.rem(mc, 2)}, device_id_type=MESH,
         )
 
-    low_shape = (rows, n_pop * PACK)
-    member_of = lax.broadcasted_iota(jnp.int32, low_shape, 0) // own_tok
-    place = lax.broadcasted_iota(jnp.int32, low_shape, 1)
-    keep = (place // PACK == member_of) & (lax.rem(place, PACK) >= RANK)
+    def far_copy(at):
+        return pltpu.make_async_remote_copy(
+            src_ref=far_out.at[at], dst_ref=far_in.at[at],
+            send_sem=far_send.at[at], recv_sem=far_recv.at[at],
+            device_id={"mp": lax.rem(mc + 2, n_mp)}, device_id_type=MESH,
+        )
 
     def project(at):
-        xa, xb = ring_a[at], ring_b[at]
-        nt = ((1,), (1,))
-        low = dot(xa, pack_a[:, :cut], nt) + dot(xb, pack_a[:, cut:], nt)
-        low = jnp.where(keep, low, 0.0)
-        y = dot(xa, wo_ref[:, :cut], nt) + dot(xb, wo_ref[:, cut:], nt)
-        for piece in split3(low):
-            y = y + dot(piece, pack_b)
-        y = y.astype(bf16)
-        for block in range(n_mp):
-            terms[at, block] = y[block * per_mp:(block + 1) * per_mp]
-
-            @pl.when(mc != block)
-            def _():
-                term_copy(at, block).start()
-
-            @pl.when(mc == block)
-            def _():
-                terms_in[block, at] = terms[at, block]
-
-    def squares(at, totals):
-        for i in range(1, n_mp):
-            source = lax.rem(mc + i, n_mp)
-            pltpu.make_async_remote_copy(
-                src_ref=terms.at[at, 0], dst_ref=terms_in.at[source, at],
-                send_sem=term_send.at[at, 0], recv_sem=term_recv.at[source, at],
-                device_id={"mp": source}, device_id_type=MESH,
-            ).wait_recv()
-        goal = target[pl.ds(pl.multiple_of(at * own_tok, own_tok), own_tok), :].astype(f32)
-        result = []
-        for k in range(members):
-            span = slice(k * own_tok, (k + 1) * own_tok)
-            out = terms_in[0, at, span].astype(f32)
-            for c in range(1, n_mp):
-                out = out + terms_in[c, at, span].astype(f32)
-            diff = out - goal
-            result.append(totals[k] + jnp.sum(diff * diff, axis=0, keepdims=True))
-        return result
-
-    project(me)
-
-    @pl.when(mc != owner)
-    def _():
-        target_copy(1).wait_recv()
-
-    totals = [jnp.zeros((1, cols), f32)] * members
-    done = [me]
-    for step in range(depth):
+        y = dot(wo_ref[...], mixed[...])
+        low = jnp.where(same, y[cols:], 0.0)
+        place = pl.ds(pl.multiple_of(at * own_tok, own_tok), own_tok)
+        more = jnp.concatenate([right_o, right_o, right_o, goal[place, :]], axis=0)
+        y = y[:cols] + dot(more, jnp.concatenate([*split3(low), pick_tok], axis=0), ((0,), (0,)))
+        terms[at] = y.reshape(terms.shape[1:]).astype(bf16)
+        near_copy(at).start()
+
+    def join(at):
+        near_copy(at).wait_recv()
+        core, side = lax.rem(mc, 2), mc // 2
+        own_sum[at] = terms[at, core, side].astype(f32) + near_in[at, side].astype(f32)
+        far_out[at] = (
+            terms[at, core, 1 - side].astype(f32) + near_in[at, 1 - side].astype(f32)
+        ).astype(bf16)
+        far_copy(at).start()
+
+    def squares(at):
+        far_copy(at).wait_recv()
+        out = own_sum[at] + far_in[at].astype(f32)
+        out = out * out
+        more = total[...]
+        for i in range(quarter // 8):
+            more = more + out[i * 8:(i + 1) * 8]
+        total[...] = more
+
+    def block_of(j):
+        away = (j + 1) // 2
+        return pop_at(my_r + jnp.where(lax.rem(j, 2) == 1, -away, away))
+
+    def arrive(j):
+        direction, step = (j - 1) % 2, (j - 1) // 2
+        if step == depth - 1:
+            for d in range(2):
+                hop(d, step, d).wait_recv()
+            return
         for g in range(2):
-            for direction in range(2):
-                if hops(direction, step, g):
-                    hop(direction, step, g).wait_recv()
-                    if hops(direction, step + 1, g):
-                        hop(direction, step + 1, g).start()
-        landed = [pop_at(my_r - 1 - step)]
-        if step < depth - 1:
-            landed.append(pop_at(my_r + 1 + step))
-        for at in landed:
-            project(at)
-        for at in done:
-            totals = squares(at, totals)
-        done = landed
-    for at in done:
-        totals = squares(at, totals)
+            hop(direction, step, g).wait_recv()
+            if hops(direction, step + 1, g):
+                hop(direction, step + 1, g).start()
+
+    def block(j, carry):
+        for k in range(1, n_pop):
+            pl.when(j == k)(functools.partial(arrive, k))
+        at = block_of(j)
+        attend(at)
+        project(at)
+
+        @pl.when(j >= 1)
+        def _():
+            join(block_of(j - 1))
+
+        @pl.when(j >= 3)
+        def _():
+            squares(block_of(j - 3))
+
+        return carry
+
+    lax.fori_loop(0, n_pop, block, 0)
+    join(block_of(n_pop - 1))
+    for j in range(n_pop - 3, n_pop):
+        squares(block_of(jnp.int32(j)))
 
     lane_row = lax.broadcasted_iota(jnp.int32, (1, 128), 1)
+    sums = jnp.sum(total[...], axis=0, keepdims=True)
+    member_of = lax.broadcasted_iota(jnp.int32, (1, rows), 1) // own_tok
     mine = jnp.zeros((1, 128), f32)
-    for k in range(members):
-        value_k = jnp.sum(totals[k], axis=1, keepdims=True)
-        mine = mine + jnp.where(lane_row == mc * members + k, value_k, 0.0)
+    for k in range(n_pop):
+        value_k = jnp.sum(jnp.where(member_of == k, sums, 0.0), axis=1, keepdims=True)
+        mine = mine + jnp.where(lane_row == k, value_k, 0.0)
 
     my_id = mc * n_pop + me
     errs[my_id] = mine
@@ -365,16 +368,9 @@
             for direction in range(2):
                 if hops(direction, step, g):
                     hop(direction, step, g).wait_send()
-    for block in range(n_mp):
-        @pl.when(mc != block)
-        def _():
-            for at in range(n_pop):
-                term_copy(at, block).wait_send()
-
-    @pl.when(mc == owner)
-    def _():
-        for i in range(1, n_mp):
-            target_copy(i).wait_send()
+    for at in range(n_pop):
+        near_copy(at).wait_send()
+        far_copy(at).wait_send()
 
     lax.fori_loop(1, n_dev, err_wait, 0)
     error = errs[0]
@@ -438,6 +434,10 @@
     own_tok = tok // n_pop
     rows = n_pop * own_tok
     cosine, sine = rope_tables(tok, HEAD_DIM)
+    half = HEAD_DIM // 2
+    by_row = lambda x: np.tile(
+        x[:, half:].T.reshape(half, n_pop, own_tok).transpose(1, 0, 2), (1, 1, 128 // own_tok)
+    )
     vmem = pl.BlockSpec(memory_space=pltpu.VMEM)
     hbm = pl.BlockSpec(memory_space=pltpu.HBM)
     smem = pl.BlockSpec(memory_space=pltpu.SMEM)
@@ -455,34 +455,42 @@
             jax.ShapeDtypeStruct((n_pop * PACK, cols), bf16),
             jax.ShapeDtypeStruct((8, 128), f32),
         ),
-        in_specs=[hbm] * 6 + [vmem] * 4 + [smem] + [vmem] * 2,
+        in_specs=[hbm] * 6 + [vmem] * 4 + [smem] + [vmem] * 4,
         out_specs=(vmem, vmem, vmem),
         scratch_shapes=[
-            like(tokens), like(w_query), like(w_key), like(w_value), like(wot), like(target),
+            like(tokens), like(w_query), pltpu.VMEM((width, 2 * HEAD_DIM), bf16),
+            pltpu.VMEM((cols + n_pop * RANK, feats), bf16), like(target),
             pltpu.VMEM((n_pop, own_tok, cut), LINK),
             pltpu.VMEM((n_pop, own_tok, feats - cut), LINK),
             pltpu.VMEM((n_pop, own_tok, cut), LINK),
             pltpu.VMEM((n_pop, own_tok, feats - cut), LINK),
-            pltpu.VMEM((n_pop, RANK, 128), bf16),
-            pltpu.VMEM((n_pop, RANK, 128), bf16),
+            pltpu.VMEM((RANK, tok), bf16),
+            pltpu.VMEM((n_pop, RANK, tok), bf16),
             pltpu.VMEM((RANK, feats), bf16),
             pltpu.VMEM((n_pop, RANK, feats), bf16),
             pltpu.VMEM((RANK, feats), bf16),
             pltpu.VMEM((n_pop, RANK, feats), bf16),
             pltpu.VMEM((n_pop, PACK, cols), bf16),
             pltpu.VMEM((n_pop, PACK, cols), bf16),
-            pltpu.VMEM((n_pop, rows, cut), bf16),
-            pltpu.VMEM((n_pop, rows, feats - cut), bf16),
-            pltpu.VMEM((n_pop, n_mp, rows // n_mp, cols), bf16),
-            pltpu.VMEM((n_mp, n_pop, rows // n_mp, cols), bf16),
+            pltpu.VMEM((n_pop, own_tok, cut), LINK),
+            pltpu.VMEM((n_pop, own_tok, feats - cut), LINK),
+            pltpu.VMEM((n_pop, tok, 2 * HEAD_DIM), bf16),
+            pltpu.VMEM((HEAD_DIM + 16, tok), bf16),
+            pltpu.VMEM((n_pop, n_pop * RANK, rows), bf16),
             pltpu.VMEM((tok, cols), bf16),
-            pltpu.VMEM((tok, cols), bf16),
+            pltpu.VMEM((feats, rows), bf16),
+            pltpu.VMEM((n_pop, 2, n_mp // 2, cols // n_mp, rows), bf16),
+            pltpu.VMEM((n_pop, n_mp // 2, cols // n_mp, rows), bf16),
+            pltpu.VMEM((n_pop, cols // n_mp, rows), bf16),
+            pltpu.VMEM((n_pop, cols // n_mp, rows), bf16),
+            pltpu.VMEM((n_pop, cols // n_mp, rows), f32),
+            pltpu.VMEM((8, rows), f32),
             pltpu.VMEM((n_dev, 1, 128), f32),
             dma((6,)),
             dma((6, n_pop)), dma((6, n_pop)),
             dma((2, depth, 2)), dma((2, depth, 2)),
-            dma((n_pop, n_mp)), dma((n_mp, n_pop)),
-            dma((n_mp,)), dma,
+            dma((n_pop,)), dma((n_pop,)),
+            dma((n_pop,)), dma((n_pop,)),
             dma((n_dev,)), dma((n_dev,)),
         ],
         compiler_params=pltpu.CompilerParams(
@@ -490,7 +498,7 @@
         ),
     )(tokens, w_query, w_key, w_value, wot, target,
       query_left_factors[0].T, query_right_factors[0], o_left[0].T, o_right[0], member_ids,
-      jnp.asarray(cosine), jnp.asarray(sine))
+      jnp.asarray(cosine), jnp.asarray(sine), jnp.asarray(by_row(cosine)), jnp.asarray(by_row(sine)))
     grad = jax.ShapeDtypeStruct((cols, feats), f32)
     grad_query, grad_out_t, fitness = pl.pallas_call(
         grad_kernel,
@@ -629,11 +637,14 @@
     tok = args[0].shape[0]
     kernel = (
         args[6].shape[0] == n_pop
+        and n_mp == 4
         and n_pop % n_mp == 0
         and n_pop % 2 == 0
         and n_pop * PACK <= 128
         and tok % (n_pop * 16) == 0
         and tok // n_pop < 128
+        and 128 % (tok // n_pop) == 0
+        and args[5].shape[1] // n_pop % (16 * n_mp) == 0
         and args[2].shape[1] // n_mp == 2 * args[5].shape[1] // n_pop
         and args[2].shape[0] == args[5].shape[1]
         and args[3].shape[1] == n_mp * HEAD_DIM

time: 76.3 us -> 70.3 us (0.921)
  Pallas kernels: 74.8 us -> 68.9 us
    pallas_call x1, Pallas kernels: 71.2 us -> 65.3 us  [per_device_fast(): pl.pallas_call(functools.partial(forward_kernel, n_pop, n_mp, width), nam...]
where the time goes in v1:
time: 70.3 us; the launch traced here: 70.2 us
  Pallas kernels  68.9 us (98%)
  between operations  1.29 us (2%)
    pallas_call x1, Pallas kernels, per_device_fast(): pl.pallas_call(functools.partial(forward_kernel, n_pop, n_mp, width), nam...  65.3 us
    pallas_call x1, Pallas kernels, per_device_fast(): pl.pallas_call(grad_kernel, name='grads', out_shape=(grad, grad, jax.Shap...  3.6 us

profile of v1, /device:TPU:0, one launch (start us, length us, event | category | flops | bytes accessed | tf_op | source)
XLA Modules:
  0.0 70.2 jit_solution(7189022377571603356)
XLA Ops:
  1.3 65.3 %forward.1 = (bf16[64,896]{1,0:T(8,128)(2,1)}, bf16[64,448]{1,0:T(8,128)(2,1)}, f32[8,128]{1,0:T(8,128)}) custom-call(bf16[256,3584]{1,0:T(8,128)(2,1)} %tok_hbm.1, bf16[448,896]{1,0:T(8,128)(2,1)} %wq_hbm.1, bf16[3584,128]{1,0:T(8,128)(2,1)} %wk_hbm.1, bf16[3584,128]{1,0:T(8,128)(2,1)} %wv_hbm.1, bf16[448,896]{1,0:T(8,128)(2,1)} %bitcast.10, ...), custom_call_target="tpu_custom_call" | custom-call | tf_op jit(solution)/shard_map/forward/pallas_call | solution.py:450
  66.6 3.6 %grads.1 = (f32[448,896]{1,0:T(8,128)}, f32[448,896]{1,0:T(8,128)}, f32[1]{0:T(128)}) custom-call(bf16[64,896]{1,0:T(8,128)(2,1)} %get-tuple-element.9.a_ref, bf16[64,448]{1,0:T(8,128)(2,1)} %get-tuple-element.10.b_ref, f32[8,128]{1,0:T(8,128)} %get-tuple-element.11.stat_ref), custom_call_target="tpu_custom_call" | custom-call | tf_op jit(solution)/shard_map/grads/pallas_call | solution.py:503

commit v2 on v1

--- a/solution.py
+++ b/solution.py
@@ -47,22 +47,21 @@
 
 def forward_kernel(
     n_pop, n_mp, width,
-    tok_hbm, wq_hbm, wk_hbm, wv_hbm, wo_hbm, tgt_hbm, ql_ref, qr_ref, ol_ref, or_ref, id_ref,
-    cos_ref, sin_ref, cos_rows, sin_rows,
+    tok_hbm, wq_hbm, wk_hbm, wv_hbm, wo_hbm, tgt_hbm, ql_hbm, qr_hbm, ol_hbm, or_hbm,
+    cos_hbm, sin_hbm, cos_rows_hbm, sin_rows_hbm, id_ref,
     pack_a_out, pack_b_out, stat_out,
-    tok_ref, wq_ref, kv_ref, wo_ref, tgt_ref,
-    part_a, part_b, parts_a, parts_b, mine_l, packs_l, mine_q, packs_q, mine_o, packs_o,
-    mine_b, packs_b, ring_a, ring_b,
-    keys, values, low_rows, goal, mixed, terms, near_in, far_out, far_in, own_sum, total, errs,
-    load_sem,
-    pop_send, pop_recv,
-    ring_send, ring_recv, near_send, near_recv, far_send, far_recv, err_send, err_recv,
+    window, wq_ref, qr_ref, tok_ref, ql_ref, ol_ref, or_ref, kv_ref, cos_ref, sin_ref,
+    tgt_ref, cos_rows, sin_rows, wo_ref,
+    part, across_in, along_out, along_in, known, mine_l, packs_l, mine_q, packs_q,
+    mine_o, packs_o, mine_b, packs_b,
+    keys, values, low_rows, goal, queries, scores, peaks, exps, mixed, terms, near_in, far_out, far_in, own_sum, total, errs,
+    load_sem, across_send, across_recv, along_send, along_recv,
+    pop_send, pop_recv, known_send, known_recv, near_send, near_recv, far_send, far_recv, err_send, err_recv,
 ):
     me = lax.axis_index("pop")
     mc = lax.axis_index("mp")
     n_dev = n_pop * n_mp
     tok, feats = tok_ref.shape[0], wq_ref.shape[1]
-    cut = ring_a.shape[2]
     own_tok = tok // n_pop
     rows = n_pop * own_tok
     heads = feats // HEAD_DIM
@@ -70,101 +69,139 @@
     ranks = n_pop * RANK
     quarter = cols // n_mp
     odd = lax.rem(me, 2) == 1
-
+    near_cols = pl.ds(pl.multiple_of(me // 2 * 2 * cols, 128), 2 * cols)
     loads = [
         pltpu.make_async_copy(src, dst, load_sem.at[i])
         for i, (src, dst) in enumerate((
-            (tok_hbm, tok_ref), (wq_hbm, wq_ref),
+            (tok_hbm.at[:, near_cols], window), (wq_hbm, wq_ref), (qr_hbm, qr_ref),
+            (tok_hbm, tok_ref), (ql_hbm, ql_ref), (ol_hbm, ol_ref), (or_hbm, or_ref),
             (wk_hbm, kv_ref.at[:, :HEAD_DIM]), (wv_hbm, kv_ref.at[:, HEAD_DIM:]),
-            (tgt_hbm, tgt_ref), (wo_hbm, wo_ref.at[:cols]),
+            (cos_hbm, cos_ref), (sin_hbm, sin_ref), (tgt_hbm, tgt_ref),
+            (cos_rows_hbm, cos_rows), (sin_rows_hbm, sin_rows), (wo_hbm, wo_ref.at[:cols]),
         ))
     ]
-    for load in loads:
+    for load in loads[:3]:
         load.start()
 
     barrier = pltpu.get_barrier_semaphore()
 
-    def greet(i, carry):
-        other = lax.rem(mc * n_pop + me + i, n_dev)
+    pops = [lax.rem(me + i, n_pop) for i in range(n_pop)]
+    mps = [lax.rem(mc + i, n_mp) for i in range(n_mp)]
+    others = [(p, m) for m in mps for p in pops][1:]
+    for p, m in others:
         pl.semaphore_signal(
-            barrier, inc=1,
-            device_id={"pop": lax.rem(other, n_pop), "mp": other // n_pop},
-            device_id_type=MESH,
+            barrier, inc=1, device_id={"pop": p, "mp": m}, device_id_type=MESH
         )
-        return carry
-
-    lax.fori_loop(1, n_dev, greet, 0)
 
     sign = 1 - 2 * lax.rem(id_ref[0], 2)
     factor = noise_scale * sign.astype(f32)
-    loads[0].wait()
-    loads[1].wait()
-    window = tok_ref[:, pl.ds(pl.multiple_of(me // 2 * 2 * cols, 128), 2 * cols)]
+    for load in loads[3:]:
+        load.start()
+    for load in loads[:3]:
+        load.wait()
     wq = wq_ref[...]
     first, second = window[:, :cols], window[:, cols:]
     base = dot(jnp.where(odd, second, first), wq)
-    part_a[...] = base[:, :cut].reshape(part_a.shape).astype(LINK)
-    part_b[...] = base[:, cut:].reshape(part_b.shape).astype(LINK)
+    for b in range(n_pop):
+        part[b % 2, b // 2] = base[b * own_tok:(b + 1) * own_tok].astype(LINK)
     mine_q[...] = (qr_ref[...].astype(f32) * factor).astype(bf16)
 
     pl.semaphore_wait(barrier, n_dev - 1)
 
-    def to_pop(i, kind):
-        other = lax.rem(me + i, n_pop)
-        src, dst = (
-            (part_a.at[other], parts_a),
-            (mine_q, packs_q),
-            (mine_l, packs_l),
-            (part_b.at[other], parts_b),
-            (mine_o, packs_o),
-            (mine_b.at[other], packs_b),
-        )[kind]
+    side, level = lax.rem(me, 2), me // 2
+    levels = n_pop // 2
+    beside = me + 1 - 2 * side
+    ways = [
+        sorted(range(levels), key=lambda t: (-abs(t - u), (t < levels // 2) == (u < levels // 2)))
+        for u in range(levels)
+    ]
+
+    def far(k):
+        at = jnp.int32(ways[0][k])
+        for u in range(1, levels):
+            at = jnp.where(level == u, ways[u][k], at)
+        return at
+
+    fars = [far(k) for k in range(levels)]
+    nears = fars[:-1][::-1]
+
+    def across(k):
         return pltpu.make_async_remote_copy(
-            src_ref=src, dst_ref=dst.at[me], send_sem=pop_send.at[kind, i],
-            recv_sem=pop_recv.at[kind, i], device_id={"pop": other}, device_id_type=MESH,
+            src_ref=part.at[1 - side, fars[k]], dst_ref=across_in.at[fars[k]],
+            send_sem=across_send, recv_sem=across_recv.at[k],
+            device_id={"pop": beside}, device_id_type=MESH,
         )
 
+    def along(k):
+        return pltpu.make_async_remote_copy(
+            src_ref=along_out.at[fars[k]], dst_ref=along_in.at[level],
+            send_sem=along_send, recv_sem=along_recv,
+            device_id={"pop": 2 * fars[k] + side}, device_id_type=MESH,
+        )
+
+    def relay(k):
+        across(k).wait_recv()
+        joined = part[side, fars[k]].astype(f32) + across_in[fars[k]].astype(f32)
+        if k == levels - 1:
+            return joined
+        along_out[fars[k]] = joined.astype(LINK)
+        along(k).start()
+
+    gathered = ((mine_q, packs_q), (mine_l, packs_l), (mine_o, packs_o), (mine_b, packs_b))
+
     def to_all(kind):
-        for i in range(1, n_pop):
-            to_pop(i, kind).start()
-
-    def from_all(kind):
-        for i in range(1, n_pop):
-            to_pop(i, kind).wait_recv()
-
+        mine, packs = gathered[kind]
+        for other in pops[1:]:
+            pltpu.make_async_remote_copy(
+                src_ref=mine.at[other] if kind == 3 else mine, dst_ref=packs.at[me],
+                send_sem=pop_send.at[kind], recv_sem=pop_recv.at[kind],
+                device_id={"pop": other}, device_id_type=MESH,
+            ).start()
+
+    def all_of(refs, send_sem, recv_sem):
+        return pltpu.make_async_remote_copy(
+            src_ref=refs, dst_ref=refs, send_sem=send_sem, recv_sem=recv_sem,
+            device_id={"pop": beside}, device_id_type=MESH,
+        )
+
+    def packs_done(kind):
+        return all_of(gathered[kind][1].at[:n_pop - 1], pop_send.at[kind], pop_recv.at[kind])
+
+    across(0).start()
     to_all(0)
-    to_all(1)
+    for k in range(1, levels):
+        across(k).start()
+    for load in loads[3:7]:
+        load.wait()
     ql = ql_ref[...]
     mine_l[...] = dot(ql, tok_ref[...], ((1,), (1,))).astype(bf16)
-    to_all(2)
-    to_all(3)
+    to_all(1)
     mine_o[...] = ol_ref[...]
     both = jnp.concatenate([ql.astype(f32), or_ref[...].astype(f32) * factor], axis=0)
     for q in range(n_pop):
         mine_b[q] = both[:, q * cols:(q + 1) * cols].astype(bf16)
-    to_all(4)
-    to_all(5)
-    for mine, packs in ((part_a, parts_a), (part_b, parts_b), (mine_b, packs_b)):
-        packs[me] = mine[me]
+    packs_b[me] = mine_b[me]
     packs_l[me] = mine_l[...]
     packs_q[me] = mine_q[...]
     packs_o[me] = mine_o[...]
 
-    loads[2].wait()
-    loads[3].wait()
+    for load in loads[7:11]:
+        load.wait()
     pair = dot(tok_ref[...], kv_ref[...])
     key = pair[:, :HEAD_DIM]
     key = (key * cos_ref[...] + pltpu.roll(key, HEAD_DIM // 2, 1) * sin_ref[...]).astype(bf16)
     values[:HEAD_DIM] = pair[:, HEAD_DIM:].T.astype(bf16)
     values[HEAD_DIM:] = jnp.ones((values.shape[0] - HEAD_DIM, tok), bf16)
+    relay(0)
     spot = lax.broadcasted_iota(jnp.int32, (tok, HEAD_DIM), 0)
     lane = lax.broadcasted_iota(jnp.int32, (tok, HEAD_DIM), 1)
     for q in range(n_pop):
         keys[q, :, :HEAD_DIM] = key
         hidden = (spot > q * own_tok + lane) & (lane < own_tok)
         keys[q, :, HEAD_DIM:] = jnp.where(hidden, -1e30, 0.0).astype(bf16)
-
-    loads[4].wait()
+    relay(1)
+
+    loads[11].wait()
     owner = me // (n_pop // n_mp)
     tgt = jnp.where(odd, tgt_ref[:, cols:], tgt_ref[:, :cols])
     goal[...] = jnp.where(mc == owner, -tgt, jnp.zeros_like(tgt))
@@ -179,8 +216,19 @@
             [p[i].astype(f32) for i in range(n_pop) for p in (parts,) + more], axis=0
         ).astype(bf16)
 
-    from_all(1)
-    from_all(2)
+    filler = jnp.zeros((keys.shape[2] - HEAD_DIM - own_tok, rows), bf16)
+    for slot in range(2):
+        for h in range(heads):
+            queries[slot, h, HEAD_DIM:HEAD_DIM + own_tok] = pick_tok
+            queries[slot, h, HEAD_DIM + own_tok:] = filler
+    total[...] = jnp.zeros_like(total)
+    for k in range(2, levels - 1):
+        relay(k)
+    own_base = relay(levels - 1)
+    to_all(2)
+    to_all(3)
+    packs_done(0).wait_recv()
+    packs_done(1).wait_recv()
     pack_q = stacked(packs_q)
     low_all = stacked(packs_l)
     spot = lax.broadcasted_iota(jnp.int32, (tok, rows), 0)
@@ -189,93 +237,82 @@
         sel = (spot == at_tok + q * own_tok).astype(bf16)
         low_rows[q] = jnp.where(same, dot(low_all, sel), 0.0).astype(bf16)
 
-    def pop_at(r):
-        r = lax.rem(r + 2 * n_pop, n_pop)
-        return jnp.where(r < n_pop // 2, 2 * r, 2 * (n_pop - 1 - r) + 1)
-
-    my_r = jnp.where(odd, n_pop - 1 - me // 2, me // 2)
-    right, left = pop_at(my_r + 1), pop_at(my_r - 1)
-
-    depth = n_pop // 2
-    rings = (ring_a, ring_b)
-
-    def hop(direction, step, g):
-        at = pop_at(my_r - step if direction == 0 else my_r + step)
+    def share(at, other):
         return pltpu.make_async_remote_copy(
-            src_ref=rings[g].at[at], dst_ref=rings[g].at[at],
-            send_sem=ring_send.at[direction, step, g], recv_sem=ring_recv.at[direction, step, g],
-            device_id={"pop": right if direction == 0 else left}, device_id_type=MESH,
+            src_ref=known.at[at], dst_ref=known.at[at],
+            send_sem=known_send, recv_sem=known_recv.at[at],
+            device_id={"pop": other}, device_id_type=MESH,
         )
 
-    def hops(direction, step, g):
-        return step < depth - 1 or (step == depth - 1 and g == direction)
-
-    for g, (kind, parts) in enumerate(((0, parts_a), (3, parts_b))):
-        from_all(kind)
-        sum_g = parts[0].astype(f32)
-        for i in range(1, n_pop):
-            sum_g = sum_g + parts[i].astype(f32)
-        rings[g][me] = sum_g.astype(LINK)
-        for direction in range(2):
-            hop(direction, 0, g).start()
-
-    from_all(4)
-    from_all(5)
-    pack_a_out[...] = stacked(packs_q, packs_o)
-    pack_b_out[...] = stacked(packs_b)
-    right_o = jnp.concatenate(
-        [packs_b[i, RANK:].astype(f32) for i in range(n_pop)], axis=0
-    ).astype(bf16)
-    loads[5].wait()
-    wo_ref[cols:] = stacked(packs_o)
-    total[...] = jnp.zeros_like(total)
+    loads[12].wait()
+    loads[13].wait()
+    all_of(along_in.at[:levels - 1], along_send, along_recv).wait_recv()
+    for k in range(levels - 1):
+        own_base = own_base + along_in[fars[k]].astype(f32)
+    known[me] = own_base.astype(LINK)
+    share(me, beside).start()
+    for near in nears:
+        share(me, 2 * near + side).start()
 
     scale = HEAD_DIM ** (-0.5) * math.log2(math.e)
     half = HEAD_DIM // 2
-    filler = jnp.zeros((keys.shape[2] - HEAD_DIM - own_tok, rows), bf16)
-
-    def attend(at):
-        cosine = jnp.concatenate([cos_rows[at]] * (rows // 128), axis=1)
-        sine = jnp.concatenate([sin_rows[at]] * (rows // 128), axis=1)
-        mix = jnp.concatenate([pick_tok, low_rows[at]], axis=0)
-        for h in range(heads):
-            lanes = slice(h * HEAD_DIM, (h + 1) * HEAD_DIM)
-            g = 0 if (h + 1) * HEAD_DIM <= cut else 1
-            here = slice(h * HEAD_DIM - g * cut, (h + 1) * HEAD_DIM - g * cut)
-            left_q = jnp.concatenate([rings[g][at, :, here], pack_q[:, lanes]], axis=0)
-            q = dot(left_q, mix, ((0,), (0,)))
-            low, high = q[:half], q[half:]
-            q = jnp.concatenate(
-                [low * cosine - high * sine, high * cosine + low * sine], axis=0
-            ).astype(bf16)
-            s = dot(keys[at], jnp.concatenate([q, pick_tok, filler], axis=0))
-            e = jnp.exp2((s - jnp.max(s, axis=0, keepdims=True)) * scale).astype(bf16)
-            out = dot(values[...], e)
-            inverse = 1.0 / out[HEAD_DIM:HEAD_DIM + 1]
-            mixed[lanes] = (out[:HEAD_DIM] * inverse).astype(bf16)
+    def attend(*group):
+        for slot, at in enumerate(group):
+            cosine = jnp.concatenate([cos_rows[at]] * (rows // 128), axis=1)
+            sine = jnp.concatenate([sin_rows[at]] * (rows // 128), axis=1)
+            mix = jnp.concatenate([pick_tok, low_rows[at]], axis=0)
+            q_all = dot(jnp.concatenate([known[at], pack_q], axis=0), mix, ((0,), (0,)))
+            for h in range(heads):
+                low = q_all[h * HEAD_DIM:h * HEAD_DIM + half]
+                high = q_all[h * HEAD_DIM + half:(h + 1) * HEAD_DIM]
+                queries[slot, h, :half] = (low * cosine - high * sine).astype(bf16)
+                queries[slot, h, half:HEAD_DIM] = (high * cosine + low * sine).astype(bf16)
+        for slot, at in enumerate(group):
+            for h in range(heads):
+                s = dot(keys[at], queries[slot, h])
+                scores[slot, h] = s
+                peak = s[:8]
+                for i in range(8, tok, 8):
+                    peak = jnp.maximum(peak, s[i:i + 8])
+                peaks[slot, h] = peak
+        for slot, at in enumerate(group):
+            for h in range(heads):
+                peak = jnp.max(peaks[slot, h], axis=0, keepdims=True)
+                exps[slot, h] = jnp.exp2((scores[slot, h] - peak) * scale).astype(bf16)
+        for slot, at in enumerate(group):
+            for h in range(heads):
+                out = dot(values[...], exps[slot, h])
+                inverse = 1.0 / out[HEAD_DIM:HEAD_DIM + 1]
+                mixed[slot, h * HEAD_DIM:(h + 1) * HEAD_DIM] = (
+                    out[:HEAD_DIM] * inverse
+                ).astype(bf16)
 
     def near_copy(at):
         return pltpu.make_async_remote_copy(
             src_ref=terms.at[at, 1 - lax.rem(mc, 2)], dst_ref=near_in.at[at],
-            send_sem=near_send.at[at], recv_sem=near_recv.at[at],
+            send_sem=near_send, recv_sem=near_recv.at[at],
             device_id={"mp": mc + 1 - 2 * lax.rem(mc, 2)}, device_id_type=MESH,
         )
 
     def far_copy(at):
         return pltpu.make_async_remote_copy(
             src_ref=far_out.at[at], dst_ref=far_in.at[at],
-            send_sem=far_send.at[at], recv_sem=far_recv.at[at],
+            send_sem=far_send, recv_sem=far_recv.at[at],
             device_id={"mp": lax.rem(mc + 2, n_mp)}, device_id_type=MESH,
         )
 
-    def project(at):
-        y = dot(wo_ref[...], mixed[...])
-        low = jnp.where(same, y[cols:], 0.0)
-        place = pl.ds(pl.multiple_of(at * own_tok, own_tok), own_tok)
-        more = jnp.concatenate([right_o, right_o, right_o, goal[place, :]], axis=0)
-        y = y[:cols] + dot(more, jnp.concatenate([*split3(low), pick_tok], axis=0), ((0,), (0,)))
-        terms[at] = y.reshape(terms.shape[1:]).astype(bf16)
-        near_copy(at).start()
+    def project(*group):
+        lows = [
+            jnp.where(same, dot(wo_ref[cols:], mixed[slot]), 0.0) for slot in range(len(group))
+        ]
+        for slot, at in enumerate(group):
+            place = pl.ds(pl.multiple_of(at * own_tok, own_tok), own_tok)
+            more = jnp.concatenate([right_o, right_o, right_o, goal[place, :]], axis=0)
+            low = jnp.concatenate([*split3(lows[slot]), pick_tok], axis=0)
+            y = dot(wo_ref[:cols], mixed[slot]) + dot(more, low, ((0,), (0,)))
+            terms[at] = y.reshape(terms.shape[1:]).astype(bf16)
+        for at in group:
+            near_copy(at).start()
 
     def join(at):
         near_copy(at).wait_recv()
@@ -295,42 +332,48 @@
             more = more + out[i * 8:(i + 1) * 8]
         total[...] = more
 
-    def block_of(j):
-        away = (j + 1) // 2
-        return pop_at(my_r + jnp.where(lax.rem(j, 2) == 1, -away, away))
-
-    def arrive(j):
-        direction, step = (j - 1) % 2, (j - 1) // 2
-        if step == depth - 1:
-            for d in range(2):
-                hop(d, step, d).wait_recv()
-            return
-        for g in range(2):
-            hop(direction, step, g).wait_recv()
-            if hops(direction, step + 1, g):
-                hop(direction, step + 1, g).start()
-
-    def block(j, carry):
-        for k in range(1, n_pop):
-            pl.when(j == k)(functools.partial(arrive, k))
-        at = block_of(j)
-        attend(at)
-        project(at)
-
-        @pl.when(j >= 1)
-        def _():
-            join(block_of(j - 1))
-
-        @pl.when(j >= 3)
-        def _():
-            squares(block_of(j - 3))
-
-        return carry
-
-    lax.fori_loop(0, n_pop, block, 0)
-    join(block_of(n_pop - 1))
-    for j in range(n_pop - 3, n_pop):
-        squares(block_of(jnp.int32(j)))
+    attend(me)
+    packs_done(2).wait_recv()
+    packs_done(3).wait_recv()
+    pack_a_out[...] = stacked(packs_q, packs_o)
+    pack_b_out[...] = stacked(packs_b)
+    right_o = jnp.concatenate(
+        [packs_b[i, RANK:].astype(f32) for i in range(n_pop)], axis=0
+    ).astype(bf16)
+    loads[14].wait()
+    wo_ref[cols:] = stacked(packs_o)
+    project(me)
+
+    def expect(at, pass_on):
+        share(at, beside).wait_recv()
+        if pass_on:
+            share(at, beside).start()
+
+    column = [2 * near + side for near in nears]
+    beyond = [2 * near + 1 - side for near in nears]
+    groups = [(me,), (beside, column[0])]
+    for i in range(1, levels - 1):
+        groups.append((column[i], beyond[i - 1]))
+    groups.append((beyond[levels - 2],))
+    expect(beside, False)
+    expect(column[0], True)
+    for k in range(1, len(groups)):
+        if k >= 2:
+            expect(beyond[k - 2], False)
+        attend(*groups[k])
+        if k < levels - 1:
+            expect(column[k], True)
+        for at in groups[k - 1]:
+            join(at)
+        project(*groups[k])
+        if k >= 2:
+            for at in groups[k - 2]:
+                squares(at)
+    for at in groups[-1]:
+        join(at)
+    for group in groups[-2:]:
+        for at in group:
+            squares(at)
 
     lane_row = lax.broadcasted_iota(jnp.int32, (1, 128), 1)
     sums = jnp.sum(total[...], axis=0, keepdims=True)
@@ -343,36 +386,20 @@
     my_id = mc * n_pop + me
     errs[my_id] = mine
 
-    def err_copy(i):
-        other = lax.rem(my_id + i, n_dev)
-        return pltpu.make_async_remote_copy(
-            src_ref=errs.at[my_id], dst_ref=errs.at[my_id],
-            send_sem=err_send.at[i], recv_sem=err_recv.at[i],
-            device_id={"pop": lax.rem(other, n_pop), "mp": other // n_pop}, device_id_type=MESH,
-        )
-
-    def err_start(i, carry):
-        err_copy(i).start()
-        return carry
-
-    def err_wait(i, carry):
-        err_copy(i).wait_recv()
-        return carry
-
-    lax.fori_loop(1, n_dev, err_start, 0)
-    for kind in range(6):
-        for i in range(1, n_pop):
-            to_pop(i, kind).wait_send()
-    for step in range(depth):
-        for g in range(2):
-            for direction in range(2):
-                if hops(direction, step, g):
-                    hop(direction, step, g).wait_send()
-    for at in range(n_pop):
-        near_copy(at).wait_send()
-        far_copy(at).wait_send()
-
-    lax.fori_loop(1, n_dev, err_wait, 0)
+    for p, m in others:
+        pltpu.make_async_remote_copy(
+            src_ref=errs.at[my_id], dst_ref=errs.at[my_id], send_sem=err_send, recv_sem=err_recv,
+            device_id={"pop": p, "mp": m}, device_id_type=MESH,
+        ).start()
+    all_errs = all_of(errs.at[:n_dev - 1], err_send, err_recv)
+    for kind in range(len(gathered)):
+        packs_done(kind).wait_send()
+    all_of(part.at[0], across_send, across_recv.at[0]).wait_send()
+    all_of(along_out.at[:levels - 1], along_send, along_recv).wait_send()
+    all_of(known.at[:n_pop - 1], known_send, known_recv.at[0]).wait_send()
+    all_of(near_in, near_send, near_recv.at[0]).wait_send()
+    all_of(far_in, far_send, far_recv.at[0]).wait_send()
+    all_errs.wait_recv()
     error = errs[0]
     for i in range(1, n_dev):
         error = error + errs[i]
@@ -386,11 +413,7 @@
         [fitness, weight, jnp.zeros((6, 128), f32)], axis=0
     )
 
-    def err_drain(i, carry):
-        err_copy(i).wait_send()
-        return carry
-
-    lax.fori_loop(1, n_dev, err_drain, 0)
+    all_errs.wait_send()
 
 
 def grad_kernel(a_ref, b_ref, stat_ref, gq_hbm, got_hbm, fit_ref, gq_ref, got_ref, sem):
@@ -442,28 +465,33 @@
     hbm = pl.BlockSpec(memory_space=pltpu.HBM)
     smem = pl.BlockSpec(memory_space=pltpu.SMEM)
     dma = pltpu.SemaphoreType.DMA
-    depth = n_pop // 2
     n_dev = n_pop * n_mp
-    cut = (feats // HEAD_DIM + 1) // 2 * HEAD_DIM
     like = lambda x: pltpu.VMEM(x.shape, x.dtype)
     wot = w_out.T
     pack_a, pack_b, stat = pl.pallas_call(
         functools.partial(forward_kernel, n_pop, n_mp, width),
         name="forward",
         out_shape=(
-            jax.ShapeDtypeStruct((n_pop * PACK, feats), bf16),
-            jax.ShapeDtypeStruct((n_pop * PACK, cols), bf16),
-            jax.ShapeDtypeStruct((8, 128), f32),
+            pltpu.VMEM((n_pop * PACK, feats), bf16),
+            pltpu.VMEM((n_pop * PACK, cols), bf16),
+            pltpu.VMEM((8, 128), f32),
         ),
-        in_specs=[hbm] * 6 + [vmem] * 4 + [smem] + [vmem] * 4,
+        in_specs=[hbm] * 14 + [smem],
         out_specs=(vmem, vmem, vmem),
         scratch_shapes=[
-            like(tokens), like(w_query), pltpu.VMEM((width, 2 * HEAD_DIM), bf16),
-            pltpu.VMEM((cols + n_pop * RANK, feats), bf16), like(target),
-            pltpu.VMEM((n_pop, own_tok, cut), LINK),
-            pltpu.VMEM((n_pop, own_tok, feats - cut), LINK),
-            pltpu.VMEM((n_pop, own_tok, cut), LINK),
-            pltpu.VMEM((n_pop, own_tok, feats - cut), LINK),
+            pltpu.VMEM((tok, 2 * cols), bf16), like(w_query), pltpu.VMEM((RANK, feats), bf16),
+            like(tokens), pltpu.VMEM((RANK, width), bf16),
+            pltpu.VMEM((RANK, feats), bf16), pltpu.VMEM((RANK, width), bf16),
+            pltpu.VMEM((width, 2 * HEAD_DIM), bf16),
+            pltpu.VMEM((tok, HEAD_DIM), f32), pltpu.VMEM((tok, HEAD_DIM), f32), like(target),
+            pltpu.VMEM((n_pop, HEAD_DIM // 2, 128), f32),
+            pltpu.VMEM((n_pop, HEAD_DIM // 2, 128), f32),
+            pltpu.VMEM((cols + n_pop * RANK, feats), bf16),
+            pltpu.VMEM((2, n_pop // 2, own_tok, feats), LINK),
+            pltpu.VMEM((n_pop // 2, own_tok, feats), LINK),
+            pltpu.VMEM((n_pop // 2, own_tok, feats), LINK),
+            pltpu.VMEM((n_pop // 2, own_tok, feats), LINK),
+            pltpu.VMEM((n_pop, own_tok, feats), LINK),
             pltpu.VMEM((RANK, tok), bf16),
             pltpu.VMEM((n_pop, RANK, tok), bf16),
             pltpu.VMEM((RANK, feats), bf16),
@@ -472,13 +500,15 @@
             pltpu.VMEM((n_pop, RANK, feats), bf16),
             pltpu.VMEM((n_pop, PACK, cols), bf16),
             pltpu.VMEM((n_pop, PACK, cols), bf16),
-            pltpu.VMEM((n_pop, own_tok, cut), LINK),
-            pltpu.VMEM((n_pop, own_tok, feats - cut), LINK),
             pltpu.VMEM((n_pop, tok, 2 * HEAD_DIM), bf16),
             pltpu.VMEM((HEAD_DIM + 16, tok), bf16),
             pltpu.VMEM((n_pop, n_pop * RANK, rows), bf16),
             pltpu.VMEM((tok, cols), bf16),
-            pltpu.VMEM((feats, rows), bf16),
+            pltpu.VMEM((2, feats // HEAD_DIM, 2 * HEAD_DIM, rows), bf16),
+            pltpu.VMEM((2, feats // HEAD_DIM, tok, rows), f32),
+            pltpu.VMEM((2, feats // HEAD_DIM, 8, rows), f32),
+            pltpu.VMEM((2, feats // HEAD_DIM, tok, rows), bf16),
+            pltpu.VMEM((2, feats, rows), bf16),
             pltpu.VMEM((n_pop, 2, n_mp // 2, cols // n_mp, rows), bf16),
             pltpu.VMEM((n_pop, n_mp // 2, cols // n_mp, rows), bf16),
             pltpu.VMEM((n_pop, cols // n_mp, rows), bf16),
@@ -486,19 +516,19 @@
             pltpu.VMEM((n_pop, cols // n_mp, rows), f32),
             pltpu.VMEM((8, rows), f32),
             pltpu.VMEM((n_dev, 1, 128), f32),
-            dma((6,)),
-            dma((6, n_pop)), dma((6, n_pop)),
-            dma((2, depth, 2)), dma((2, depth, 2)),
-            dma((n_pop,)), dma((n_pop,)),
-            dma((n_pop,)), dma((n_pop,)),
-            dma((n_dev,)), dma((n_dev,)),
+            dma((15,)),
+            dma, dma((n_pop // 2,)), dma, dma,
+            dma((4,)), dma((4,)), dma, dma((n_pop,)),
+            dma, dma((n_pop,)), dma, dma((n_pop,)),
+            dma, dma,
         ],
         compiler_params=pltpu.CompilerParams(
             collective_id=0, has_side_effects=True, vmem_limit_bytes=60 * 1024 * 1024
         ),
     )(tokens, w_query, w_key, w_value, wot, target,
-      query_left_factors[0].T, query_right_factors[0], o_left[0].T, o_right[0], member_ids,
-      jnp.asarray(cosine), jnp.asarray(sine), jnp.asarray(by_row(cosine)), jnp.asarray(by_row(sine)))
+      query_left_factors[0].T, query_right_factors[0], o_left[0].T, o_right[0],
+      jnp.asarray(cosine), jnp.asarray(sine), jnp.asarray(by_row(cosine)), jnp.asarray(by_row(sine)),
+      member_ids)
     grad = jax.ShapeDtypeStruct((cols, feats), f32)
     grad_query, grad_out_t, fitness = pl.pallas_call(
         grad_kernel,
@@ -507,6 +537,7 @@
         in_specs=[vmem, vmem, vmem],
         out_specs=(hbm, hbm, smem),
         scratch_shapes=[like(grad), like(grad), dma((4,))],
+        compiler_params=pltpu.CompilerParams(vmem_limit_bytes=16 * 1024 * 1024),
     )(pack_a, pack_b, stat)
     return grad_query, grad_out_t.T, fitness
 

time: 70.3 us -> 48.3 us (0.69)
  Pallas kernels: 68.9 us -> 46.9 us
    pallas_call x1, Pallas kernels: 65.3 us -> 44.2 us  [per_device_fast(): pl.pallas_call(functools.partial(forward_kernel, n_pop, n_mp, width), nam...]
    pallas_call x1, Pallas kernels: 3.6 us -> 2.66 us  [per_device_fast(): pl.pallas_call(grad_kernel, name='grads', out_shape=(grad, grad, jax.Shap...]
where the time goes in v2:
time: 48.3 us; the launch traced here: 48.2 us
  Pallas kernels  46.9 us (97%)
  between operations  1.29 us (3%)
    pallas_call x1, Pallas kernels, per_device_fast(): pl.pallas_call(functools.partial(forward_kernel, n_pop, n_mp, width), nam...  44.2 us
    pallas_call x1, Pallas kernels, per_device_fast(): pl.pallas_call(grad_kernel, name='grads', out_shape=(grad, grad, jax.Shap...  2.66 us

profile of v2, /device:TPU:0, one launch (start us, length us, event | category | flops | bytes accessed | tf_op | source)
XLA Modules:
  0.0 48.2 jit_solution(15528858711219974663)
XLA Ops:
  1.3 44.2 %forward.1 = (bf16[64,896]{1,0:T(8,128)(2,1)S(1)}, bf16[64,448]{1,0:T(8,128)(2,1)S(1)}, f32[8,128]{1,0:T(8,128)S(1)}) custom-call(bf16[256,3584]{1,0:T(8,128)(2,1)} %tok_hbm.1, bf16[448,896]{1,0:T(8,128)(2,1)} %wq_hbm.1, bf16[3584,128]{1,0:T(8,128)(2,1)} %wk_hbm.1, bf16[3584,128]{1,0:T(8,128)(2,1)} %wv_hbm.1, bf16[448,896]{1,0:T(8,128)(2,1)} %bitcast.10, ...), custom_call_target="tpu_custom_call" | custom-call | tf_op jit(solution)/shard_map/forward/pallas_call | solution.py:471
  45.5 2.7 %grads.1 = (f32[448,896]{1,0:T(8,128)}, f32[448,896]{1,0:T(8,128)}, f32[1]{0:T(128)}) custom-call(bf16[64,896]{1,0:T(8,128)(2,1)S(1)} %get-tuple-element.9.a_ref, bf16[64,448]{1,0:T(8,128)(2,1)S(1)} %get-tuple-element.10.b_ref, f32[8,128]{1,0:T(8,128)S(1)} %get-tuple-element.11.stat_ref), custom_call_target="tpu_custom_call" | custom-call | tf_op jit(solution)/shard_map/grads/pallas_call | solution.py:533

commit v3 on v2

--- a/solution.py
+++ b/solution.py
@@ -48,12 +48,12 @@
 def forward_kernel(
     n_pop, n_mp, width,
     tok_hbm, wq_hbm, wk_hbm, wv_hbm, wo_hbm, tgt_hbm, ql_hbm, qr_hbm, ol_hbm, or_hbm,
-    cos_hbm, sin_hbm, cos_rows_hbm, sin_rows_hbm, id_ref,
-    pack_a_out, pack_b_out, stat_out,
-    window, wq_ref, qr_ref, tok_ref, ql_ref, ol_ref, or_ref, kv_ref, cos_ref, sin_ref,
+    cos_hbm, sin_hbm, cos_rows_hbm, sin_rows_hbm, id_hbm,
+    rows_out, left_out, stat_out,
+    id_ref, window, wq_ref, qr_ref, tok_ref, ql_ref, ol_ref, or_ref, kv_ref, cos_ref, sin_ref,
     tgt_ref, cos_rows, sin_rows, wo_ref,
-    part, across_in, along_out, along_in, known, mine_l, packs_l, mine_q, packs_q,
-    mine_o, packs_o, mine_b, packs_b,
+    part, across_in, along_out, along_in, own_base, known, mine_l, packs_l, mine_q, packs_q,
+    mine_o, packs_o, mine_b, packs_b, mine_a, packs_a,
     keys, values, low_rows, goal, queries, scores, peaks, exps, mixed, terms, near_in, far_out, far_in, own_sum, total, errs,
     load_sem, across_send, across_recv, along_send, along_recv,
     pop_send, pop_recv, known_send, known_recv, near_send, near_recv, far_send, far_recv, err_send, err_recv,
@@ -65,22 +65,25 @@
     own_tok = tok // n_pop
     rows = n_pop * own_tok
     heads = feats // HEAD_DIM
-    cols = wq_ref.shape[0]
+    cols = wo_hbm.shape[0]
     ranks = n_pop * RANK
     quarter = cols // n_mp
     odd = lax.rem(me, 2) == 1
-    near_cols = pl.ds(pl.multiple_of(me // 2 * 2 * cols, 128), 2 * cols)
+    lead = wq_ref.shape[0] - cols
+    near_cols = pl.ds(pl.multiple_of(me * cols - jnp.where(odd, lead, 0), 128), cols + lead)
+    near_rows = pl.ds(pl.multiple_of(jnp.where(odd, lead, 0), 16), cols)
     loads = [
         pltpu.make_async_copy(src, dst, load_sem.at[i])
         for i, (src, dst) in enumerate((
-            (tok_hbm.at[:, near_cols], window), (wq_hbm, wq_ref), (qr_hbm, qr_ref),
+            (tok_hbm.at[:, near_cols], window), (wq_hbm, wq_ref.at[near_rows]), (qr_hbm, qr_ref),
             (tok_hbm, tok_ref), (ql_hbm, ql_ref), (ol_hbm, ol_ref), (or_hbm, or_ref),
             (wk_hbm, kv_ref.at[:, :HEAD_DIM]), (wv_hbm, kv_ref.at[:, HEAD_DIM:]),
             (cos_hbm, cos_ref), (sin_hbm, sin_ref), (tgt_hbm, tgt_ref),
             (cos_rows_hbm, cos_rows), (sin_rows_hbm, sin_rows), (wo_hbm, wo_ref.at[:cols]),
+            (id_hbm, id_ref),
         ))
     ]
-    for load in loads[:3]:
+    for load in loads[:3] + loads[15:]:
         load.start()
 
     barrier = pltpu.get_barrier_semaphore()
@@ -88,29 +91,34 @@
     pops = [lax.rem(me + i, n_pop) for i in range(n_pop)]
     mps = [lax.rem(mc + i, n_mp) for i in range(n_mp)]
     others = [(p, m) for m in mps for p in pops][1:]
-    for p, m in others:
+    side, level = lax.rem(me, 2), me // 2
+    levels = n_pop // 2
+    beside = me + 1 - 2 * side
+    aligned = [2 * lax.rem(level + i, levels) + side for i in range(1, levels)]
+    near_mp, far_mp = mc + 1 - 2 * lax.rem(mc, 2), lax.rem(mc + 2, n_mp)
+    partners = [(p, mc) for p in aligned[::-1] + [beside]] + [(me, near_mp), (me, far_mp)]
+    for p, m in partners:
         pl.semaphore_signal(
             barrier, inc=1, device_id={"pop": p, "mp": m}, device_id_type=MESH
         )
 
+    if lead:
+        wq_ref[pl.ds(pl.multiple_of(jnp.where(odd, 0, cols), 16), lead), :] = jnp.zeros(
+            (lead, feats), bf16
+        )
+    for load in loads[3:15]:
+        load.start()
+    for load in loads[:3] + loads[15:]:
+        load.wait()
     sign = 1 - 2 * lax.rem(id_ref[0], 2)
     factor = noise_scale * sign.astype(f32)
-    for load in loads[3:]:
-        load.start()
-    for load in loads[:3]:
-        load.wait()
-    wq = wq_ref[...]
-    first, second = window[:, :cols], window[:, cols:]
-    base = dot(jnp.where(odd, second, first), wq)
+    base = dot(window[...], wq_ref[...])
     for b in range(n_pop):
         part[b % 2, b // 2] = base[b * own_tok:(b + 1) * own_tok].astype(LINK)
     mine_q[...] = (qr_ref[...].astype(f32) * factor).astype(bf16)
 
-    pl.semaphore_wait(barrier, n_dev - 1)
-
-    side, level = lax.rem(me, 2), me // 2
-    levels = n_pop // 2
-    beside = me + 1 - 2 * side
+    pl.semaphore_wait(barrier, len(partners))
+
     ways = [
         sorted(range(levels), key=lambda t: (-abs(t - u), (t < levels // 2) == (u < levels // 2)))
         for u in range(levels)
@@ -125,35 +133,46 @@
     fars = [far(k) for k in range(levels)]
     nears = fars[:-1][::-1]
 
-    def across(k):
+    cut = (heads + 1) // 2 * HEAD_DIM
+    halves = (slice(0, cut), slice(cut, feats))
+
+    def across(k, g):
         return pltpu.make_async_remote_copy(
-            src_ref=part.at[1 - side, fars[k]], dst_ref=across_in.at[fars[k]],
-            send_sem=across_send, recv_sem=across_recv.at[k],
+            src_ref=part.at[1 - side, fars[k], :, halves[g]],
+            dst_ref=across_in.at[fars[k], :, halves[g]],
+            send_sem=across_send, recv_sem=across_recv.at[k, g],
             device_id={"pop": beside}, device_id_type=MESH,
         )
 
-    def along(k):
+    def along(k, g):
         return pltpu.make_async_remote_copy(
-            src_ref=along_out.at[fars[k]], dst_ref=along_in.at[level],
+            src_ref=along_out.at[fars[k], :, halves[g]],
+            dst_ref=along_in.at[level, :, halves[g]],
             send_sem=along_send, recv_sem=along_recv,
             device_id={"pop": 2 * fars[k] + side}, device_id_type=MESH,
         )
 
     def relay(k):
-        across(k).wait_recv()
-        joined = part[side, fars[k]].astype(f32) + across_in[fars[k]].astype(f32)
-        if k == levels - 1:
-            return joined
-        along_out[fars[k]] = joined.astype(LINK)
-        along(k).start()
-
-    gathered = ((mine_q, packs_q), (mine_l, packs_l), (mine_o, packs_o), (mine_b, packs_b))
-
-    def to_all(kind):
+        for g, lanes in enumerate(halves):
+            across(k, g).wait_recv()
+            joined = part[side, fars[k], :, lanes].astype(f32)
+            joined = joined + across_in[fars[k], :, lanes].astype(f32)
+            if k == levels - 1:
+                own_base[:, lanes] = joined
+            else:
+                along_out[fars[k], :, lanes] = joined.astype(LINK)
+                along(k, g).start()
+
+    gathered = ((mine_q, packs_q), (mine_l, packs_l), (mine_o, packs_o), (mine_b, packs_b),
+                (mine_a, packs_a))
+
+    crossed = [2 * lax.rem(level + i, levels) + 1 - side for i in range(levels)]
+
+    def give(kind, places):
         mine, packs = gathered[kind]
-        for other in pops[1:]:
+        for other in places:
             pltpu.make_async_remote_copy(
-                src_ref=mine.at[other] if kind == 3 else mine, dst_ref=packs.at[me],
+                src_ref=mine.at[other] if kind >= 3 else mine, dst_ref=packs.at[me],
                 send_sem=pop_send.at[kind], recv_sem=pop_recv.at[kind],
                 device_id={"pop": other}, device_id_type=MESH,
             ).start()
@@ -167,20 +186,26 @@
     def packs_done(kind):
         return all_of(gathered[kind][1].at[:n_pop - 1], pop_send.at[kind], pop_recv.at[kind])
 
-    across(0).start()
-    to_all(0)
+    for g in range(2):
+        across(0, g).start()
+    give(0, aligned)
     for k in range(1, levels):
-        across(k).start()
+        for g in range(2):
+            across(k, g).start()
     for load in loads[3:7]:
         load.wait()
     ql = ql_ref[...]
     mine_l[...] = dot(ql, tok_ref[...], ((1,), (1,))).astype(bf16)
-    to_all(1)
+    give(1, aligned)
     mine_o[...] = ol_ref[...]
-    both = jnp.concatenate([ql.astype(f32), or_ref[...].astype(f32) * factor], axis=0)
+    scaled = (or_ref[...].astype(f32) * factor).astype(bf16)
     for q in range(n_pop):
-        mine_b[q] = both[:, q * cols:(q + 1) * cols].astype(bf16)
+        mine_a[q] = ql[:, q * cols:(q + 1) * cols]
+        mine_b[q] = scaled[:, q * cols:(q + 1) * cols]
+    give(2, aligned)
+    give(3, aligned)
     packs_b[me] = mine_b[me]
+    packs_a[me] = mine_a[me]
     packs_l[me] = mine_l[...]
     packs_q[me] = mine_q[...]
     packs_o[me] = mine_o[...]
@@ -193,6 +218,8 @@
     values[:HEAD_DIM] = pair[:, HEAD_DIM:].T.astype(bf16)
     values[HEAD_DIM:] = jnp.ones((values.shape[0] - HEAD_DIM, tok), bf16)
     relay(0)
+    give(0, crossed)
+    give(1, crossed)
     spot = lax.broadcasted_iota(jnp.int32, (tok, HEAD_DIM), 0)
     lane = lax.broadcasted_iota(jnp.int32, (tok, HEAD_DIM), 1)
     for q in range(n_pop):
@@ -224,9 +251,7 @@
     total[...] = jnp.zeros_like(total)
     for k in range(2, levels - 1):
         relay(k)
-    own_base = relay(levels - 1)
-    to_all(2)
-    to_all(3)
+    relay(levels - 1)
     packs_done(0).wait_recv()
     packs_done(1).wait_recv()
     pack_q = stacked(packs_q)
@@ -247,16 +272,20 @@
     loads[12].wait()
     loads[13].wait()
     all_of(along_in.at[:levels - 1], along_send, along_recv).wait_recv()
+    own = own_base[...]
     for k in range(levels - 1):
-        own_base = own_base + along_in[fars[k]].astype(f32)
-    known[me] = own_base.astype(LINK)
+        own = own + along_in[fars[k]].astype(f32)
+    known[me] = own.astype(LINK)
     share(me, beside).start()
-    for near in nears:
+    share(me, 2 * nears[0] + side).start()
+    give(2, crossed)
+    give(3, crossed)
+    for near in nears[1:]:
         share(me, 2 * near + side).start()
 
     scale = HEAD_DIM ** (-0.5) * math.log2(math.e)
     half = HEAD_DIM // 2
-    def attend(*group):
+    def attend(group, first=0):
         for slot, at in enumerate(group):
             cosine = jnp.concatenate([cos_rows[at]] * (rows // 128), axis=1)
             sine = jnp.concatenate([sin_rows[at]] * (rows // 128), axis=1)
@@ -283,7 +312,7 @@
             for h in range(heads):
                 out = dot(values[...], exps[slot, h])
                 inverse = 1.0 / out[HEAD_DIM:HEAD_DIM + 1]
-                mixed[slot, h * HEAD_DIM:(h + 1) * HEAD_DIM] = (
+                mixed[first + slot, h * HEAD_DIM:(h + 1) * HEAD_DIM] = (
                     out[:HEAD_DIM] * inverse
                 ).astype(bf16)
 
@@ -291,24 +320,22 @@
         return pltpu.make_async_remote_copy(
             src_ref=terms.at[at, 1 - lax.rem(mc, 2)], dst_ref=near_in.at[at],
             send_sem=near_send, recv_sem=near_recv.at[at],
-            device_id={"mp": mc + 1 - 2 * lax.rem(mc, 2)}, device_id_type=MESH,
+            device_id={"mp": near_mp}, device_id_type=MESH,
         )
 
     def far_copy(at):
         return pltpu.make_async_remote_copy(
             src_ref=far_out.at[at], dst_ref=far_in.at[at],
             send_sem=far_send, recv_sem=far_recv.at[at],
-            device_id={"mp": lax.rem(mc + 2, n_mp)}, device_id_type=MESH,
-        )
-
-    def project(*group):
-        lows = [
-            jnp.where(same, dot(wo_ref[cols:], mixed[slot]), 0.0) for slot in range(len(group))
-        ]
-        for slot, at in enumerate(group):
+            device_id={"mp": far_mp}, device_id_type=MESH,
+        )
+
+    def project(group, slots):
+        lows = [jnp.where(same, dot(wo_ref[cols:], mixed[slot]), 0.0) for slot in slots]
+        for slot, at, low in zip(slots, group, lows):
             place = pl.ds(pl.multiple_of(at * own_tok, own_tok), own_tok)
             more = jnp.concatenate([right_o, right_o, right_o, goal[place, :]], axis=0)
-            low = jnp.concatenate([*split3(lows[slot]), pick_tok], axis=0)
+            low = jnp.concatenate([*split3(low), pick_tok], axis=0)
             y = dot(wo_ref[:cols], mixed[slot]) + dot(more, low, ((0,), (0,)))
             terms[at] = y.reshape(terms.shape[1:]).astype(bf16)
         for at in group:
@@ -332,17 +359,7 @@
             more = more + out[i * 8:(i + 1) * 8]
         total[...] = more
 
-    attend(me)
-    packs_done(2).wait_recv()
-    packs_done(3).wait_recv()
-    pack_a_out[...] = stacked(packs_q, packs_o)
-    pack_b_out[...] = stacked(packs_b)
-    right_o = jnp.concatenate(
-        [packs_b[i, RANK:].astype(f32) for i in range(n_pop)], axis=0
-    ).astype(bf16)
-    loads[14].wait()
-    wo_ref[cols:] = stacked(packs_o)
-    project(me)
+    attend((me,), 2)
 
     def expect(at, pass_on):
         share(at, beside).wait_recv()
@@ -357,21 +374,32 @@
     groups.append((beyond[levels - 2],))
     expect(beside, False)
     expect(column[0], True)
+    attend(groups[1])
+    packs_done(2).wait_recv()
+    packs_done(3).wait_recv()
+    right_o = jnp.concatenate(
+        [packs_b[i].astype(f32) for i in range(n_pop)], axis=0
+    ).astype(bf16)
+    loads[14].wait()
+    pack_o = stacked(packs_o)
+    wo_ref[cols:] = pack_o
+    project(groups[0] + groups[1], (2, 0, 1))
+    give(4, aligned + crossed)
+    expect(column[1], True)
+    groups = [groups[0] + groups[1]] + groups[2:]
     for k in range(1, len(groups)):
-        if k >= 2:
-            expect(beyond[k - 2], False)
-        attend(*groups[k])
-        if k < levels - 1:
-            expect(column[k], True)
+        expect(beyond[k - 1], False)
+        attend(groups[k])
+        if k + 1 < levels - 1:
+            expect(column[k + 1], True)
         for at in groups[k - 1]:
             join(at)
-        project(*groups[k])
-        if k >= 2:
-            for at in groups[k - 2]:
-                squares(at)
+        project(groups[k], range(len(groups[k])))
+    for at in groups[0]:
+        squares(at)
     for at in groups[-1]:
         join(at)
-    for group in groups[-2:]:
+    for group in groups[1:]:
         for at in group:
             squares(at)
 
@@ -394,11 +422,21 @@
     all_errs = all_of(errs.at[:n_dev - 1], err_send, err_recv)
     for kind in range(len(gathered)):
         packs_done(kind).wait_send()
-    all_of(part.at[0], across_send, across_recv.at[0]).wait_send()
+    all_of(part.at[0], across_send, across_recv.at[0, 0]).wait_send()
     all_of(along_out.at[:levels - 1], along_send, along_recv).wait_send()
     all_of(known.at[:n_pop - 1], known_send, known_recv.at[0]).wait_send()
     all_of(near_in, near_send, near_recv.at[0]).wait_send()
     all_of(far_in, far_send, far_recv.at[0]).wait_send()
+    rows_out[0] = pack_q
+    rows_out[1] = pack_o
+    packs_done(4).wait_recv()
+    for i, packs in enumerate((packs_a, packs_b)):
+        some = jnp.concatenate([packs[j].astype(f32) for j in range(n_pop)], axis=0)
+        some = jnp.concatenate([some] * 3 + [jnp.zeros((left_out.shape[2] - 3 * ranks, cols), f32)], axis=0)
+        some = jnp.concatenate(
+            [some, jnp.zeros((some.shape[0], left_out.shape[1] - cols), f32)], axis=1
+        )
+        left_out[i] = some.T.astype(bf16)
     all_errs.wait_recv()
     error = errs[0]
     for i in range(1, n_dev):
@@ -416,32 +454,30 @@
     all_errs.wait_send()
 
 
-def grad_kernel(a_ref, b_ref, stat_ref, gq_hbm, got_hbm, fit_ref, gq_ref, got_ref, sem):
-    pack_a = a_ref[...]
-    pack_b = b_ref[...].astype(f32)
-    rows, cols = pack_b.shape
-    row = lax.broadcasted_iota(jnp.int32, (rows, 128), 0)
-    lane = lax.broadcasted_iota(jnp.int32, (rows, 128), 1)
-    per_row = jnp.sum(jnp.where(lane == row // PACK, stat_ref[1:2, :], 0.0), axis=1, keepdims=True)
-    per_row = per_row / (noise_scale * noise_scale)
-    kind = lax.rem(lax.broadcasted_iota(jnp.int32, (rows, 1), 0), PACK)
-    edges = (0, (cols // 2 + 127) // 128 * 128, cols)
+def grad_kernel(rows_ref, left_ref, stat_ref, gq_hbm, got_hbm, fit_hbm, gq_ref, got_ref, fit_ref, sem, fit_sem):
+    ranks, feats = rows_ref.shape[1:]
+    cols = gq_ref.shape[0]
+    row = lax.broadcasted_iota(jnp.int32, (ranks, 128), 0)
+    lane = lax.broadcasted_iota(jnp.int32, (ranks, 128), 1)
+    weight = jnp.sum(jnp.where(lane == row // RANK, stat_ref[1:2, :], 0.0), axis=1, keepdims=True)
+    weight = weight / (noise_scale * noise_scale)
+    filler = jnp.zeros((left_ref.shape[2] - 3 * ranks, feats), bf16)
+    step = cols // (sem.shape[0] // 2)
     copies = []
-    for out, target, weight in (
-        (gq_ref, gq_hbm, jnp.where(kind < RANK, per_row, 0.0)),
-        (got_ref, got_hbm, jnp.where(kind >= RANK, per_row, 0.0)),
-    ):
-        pieces = jnp.concatenate(split3(pack_b * weight), axis=0)
-        right = jnp.concatenate([pack_a] * 3, axis=0)
-        for low, high in zip(edges[:-1], edges[1:]):
-            out[low:high, :] = dot(pieces[:, low:high], right, ((0,), (0,)))
+    for i, (out, target) in enumerate(((gq_ref, gq_hbm), (got_ref, got_hbm))):
+        right = jnp.concatenate([*split3(rows_ref[i].astype(f32) * weight), filler], axis=0)
+        for low in range(0, cols, step):
+            out[low:low + step, :] = dot(left_ref[i, low:low + step, :], right)
             copy = pltpu.make_async_copy(
-                out.at[low:high], target.at[low:high], sem.at[len(copies)]
+                out.at[low:low + step], target.at[low:low + step], sem.at[len(copies)]
             )
             copy.start()
             copies.append(copy)
     me = lax.axis_index("pop")
     fit_ref[0] = jnp.sum(jnp.where(lane[:1] == me, stat_ref[0:1, :], 0.0))
+    copy = pltpu.make_async_copy(fit_ref, fit_hbm, fit_sem)
+    copy.start()
+    copies.append(copy)
     for copy in copies:
         copy.wait()
 
@@ -463,23 +499,22 @@
     )
     vmem = pl.BlockSpec(memory_space=pltpu.VMEM)
     hbm = pl.BlockSpec(memory_space=pltpu.HBM)
-    smem = pl.BlockSpec(memory_space=pltpu.SMEM)
     dma = pltpu.SemaphoreType.DMA
     n_dev = n_pop * n_mp
     like = lambda x: pltpu.VMEM(x.shape, x.dtype)
     wot = w_out.T
-    pack_a, pack_b, stat = pl.pallas_call(
+    packs, left, stat = pl.pallas_call(
         functools.partial(forward_kernel, n_pop, n_mp, width),
         name="forward",
         out_shape=(
-            pltpu.VMEM((n_pop * PACK, feats), bf16),
-            pltpu.VMEM((n_pop * PACK, cols), bf16),
+            pltpu.VMEM((2, n_pop * RANK, feats), bf16),
+            pltpu.VMEM((2, -(-cols // 128) * 128, n_pop * PACK * 2), bf16),
             pltpu.VMEM((8, 128), f32),
         ),
-        in_specs=[hbm] * 14 + [smem],
+        in_specs=[hbm] * 15,
         out_specs=(vmem, vmem, vmem),
         scratch_shapes=[
-            pltpu.VMEM((tok, 2 * cols), bf16), like(w_query), pltpu.VMEM((RANK, feats), bf16),
+            pltpu.SMEM((1,), jnp.int32), pltpu.VMEM((tok, cols + cols % 128), bf16), pltpu.VMEM((cols + cols % 128, feats), bf16), pltpu.VMEM((RANK, feats), bf16),
             like(tokens), pltpu.VMEM((RANK, width), bf16),
             pltpu.VMEM((RANK, feats), bf16), pltpu.VMEM((RANK, width), bf16),
             pltpu.VMEM((width, 2 * HEAD_DIM), bf16),
@@ -491,6 +526,7 @@
             pltpu.VMEM((n_pop // 2, own_tok, feats), LINK),
             pltpu.VMEM((n_pop // 2, own_tok, feats), LINK),
             pltpu.VMEM((n_pop // 2, own_tok, feats), LINK),
+            pltpu.VMEM((own_tok, feats), f32),
             pltpu.VMEM((n_pop, own_tok, feats), LINK),
             pltpu.VMEM((RANK, tok), bf16),
             pltpu.VMEM((n_pop, RANK, tok), bf16),
@@ -498,8 +534,10 @@
             pltpu.VMEM((n_pop, RANK, feats), bf16),
             pltpu.VMEM((RANK, feats), bf16),
             pltpu.VMEM((n_pop, RANK, feats), bf16),
-            pltpu.VMEM((n_pop, PACK, cols), bf16),
-            pltpu.VMEM((n_pop, PACK, cols), bf16),
+            pltpu.VMEM((n_pop, RANK, cols), bf16),
+            pltpu.VMEM((n_pop, RANK, cols), bf16),
+            pltpu.VMEM((n_pop, RANK, cols), bf16),
+            pltpu.VMEM((n_pop, RANK, cols), bf16),
             pltpu.VMEM((n_pop, tok, 2 * HEAD_DIM), bf16),
             pltpu.VMEM((HEAD_DIM + 16, tok), bf16),
             pltpu.VMEM((n_pop, n_pop * RANK, rows), bf16),
@@ -508,7 +546,7 @@
             pltpu.VMEM((2, feats // HEAD_DIM, tok, rows), f32),
             pltpu.VMEM((2, feats // HEAD_DIM, 8, rows), f32),
             pltpu.VMEM((2, feats // HEAD_DIM, tok, rows), bf16),
-            pltpu.VMEM((2, feats, rows), bf16),
+            pltpu.VMEM((3, feats, rows), bf16),
             pltpu.VMEM((n_pop, 2, n_mp // 2, cols // n_mp, rows), bf16),
             pltpu.VMEM((n_pop, n_mp // 2, cols // n_mp, rows), bf16),
             pltpu.VMEM((n_pop, cols // n_mp, rows), bf16),
@@ -516,9 +554,9 @@
             pltpu.VMEM((n_pop, cols // n_mp, rows), f32),
             pltpu.VMEM((8, rows), f32),
             pltpu.VMEM((n_dev, 1, 128), f32),
-            dma((15,)),
-            dma, dma((n_pop // 2,)), dma, dma,
-            dma((4,)), dma((4,)), dma, dma((n_pop,)),
+            dma((16,)),
+            dma, dma((n_pop // 2, 2)), dma, dma,
+            dma((5,)), dma((5,)), dma, dma((n_pop,)),
             dma, dma((n_pop,)), dma, dma((n_pop,)),
             dma, dma,
         ],
@@ -535,10 +573,10 @@
         name="grads",
         out_shape=(grad, grad, jax.ShapeDtypeStruct((1,), f32)),
         in_specs=[vmem, vmem, vmem],
-        out_specs=(hbm, hbm, smem),
-        scratch_shapes=[like(grad), like(grad), dma((4,))],
+        out_specs=(hbm, hbm, hbm),
+        scratch_shapes=[like(grad), like(grad), pltpu.SMEM((1,), f32), dma((8,)), dma],
         compiler_params=pltpu.CompilerParams(vmem_limit_bytes=16 * 1024 * 1024),
-    )(pack_a, pack_b, stat)
+    )(packs, left, stat)
     return grad_query, grad_out_t.T, fitness
 
 
@@ -676,6 +714,8 @@
         and tok // n_pop < 128
         and 128 % (tok // n_pop) == 0
         and args[5].shape[1] // n_pop % (16 * n_mp) == 0
+        and n_pop >= 8
+        and n_pop * PACK * 2 % 128 == 0
         and args[2].shape[1] // n_mp == 2 * args[5].shape[1] // n_pop
         and args[2].shape[0] == args[5].shape[1]
         and args[3].shape[1] == n_mp * HEAD_DIM

time: 48.3 us -> 45.5 us (0.942)
  Pallas kernels: 46.9 us -> 44 us
    pallas_call x1, Pallas kernels: 44.2 us -> 42 us  [per_device_fast(): pl.pallas_call(functools.partial(forward_kernel, n_pop, n_mp, width), nam...]
    pallas_call x1, Pallas kernels: 2.66 us -> 2.06 us  [per_device_fast(): pl.pallas_call(grad_kernel, name='grads', out_shape=(grad, grad, jax.Shap...]
where the time goes in v3:
time: 45.5 us; the launch traced here: 45.3 us
  Pallas kernels  44 us (97%)
  between operations  1.29 us (3%)
    pallas_call x1, Pallas kernels, per_device_fast(): pl.pallas_call(functools.partial(forward_kernel, n_pop, n_mp, width), nam...  42 us
    pallas_call x1, Pallas kernels, per_device_fast(): pl.pallas_call(grad_kernel, name='grads', out_shape=(grad, grad, jax.Shap...  2.06 us

profile of v3, /device:TPU:0, one launch (start us, length us, event | category | flops | bytes accessed | tf_op | source)
XLA Modules:
  0.0 45.3 jit_solution(6285717686512858056)
XLA Ops:
  1.3 42.0 %forward.1 = (bf16[2,32,896]{2,1,0:T(8,128)(2,1)S(1)}, bf16[2,512,128]{2,1,0:T(8,128)(2,1)S(1)}, f32[8,128]{1,0:T(8,128)S(1)}) custom-call(bf16[256,3584]{1,0:T(8,128)(2,1)} %tok_hbm.1, bf16[448,896]{1,0:T(8,128)(2,1)} %wq_hbm.1, bf16[3584,128]{1,0:T(8,128)(2,1)} %wk_hbm.1, bf16[3584,128]{1,0:T(8,128)(2,1)} %wv_hbm.1, bf16[448,896]{1,0:T(8,128)(2,1)} %bitcast.10, ...), custom_call_target="tpu_custom_call" | custom-call | tf_op jit(solution)/shard_map/forward/pallas_call | solution.py:506
  43.3 2.1 %grads.1 = (f32[448,896]{1,0:T(8,128)}, f32[448,896]{1,0:T(8,128)}, f32[1]{0:T(128)}) custom-call(bf16[2,32,896]{2,1,0:T(8,128)(2,1)S(1)} %get-tuple-element.9.rows_ref, bf16[2,512,128]{2,1,0:T(8,128)(2,1)S(1)} %get-tuple-element.10.left_ref, f32[8,128]{1,0:T(8,128)S(1)} %get-tuple-element.11.stat_ref), custom_call_target="tpu_custom_call" | custom-call | tf_op jit(solution)/shard_map/grads/pallas_call | solution.py:571

commit v4 on v3

--- a/solution.py
+++ b/solution.py
@@ -55,7 +55,7 @@
     part, across_in, along_out, along_in, own_base, known, mine_l, packs_l, mine_q, packs_q,
     mine_o, packs_o, mine_b, packs_b, mine_a, packs_a,
     keys, values, low_rows, goal, queries, scores, peaks, exps, mixed, terms, near_in, far_out, far_in, own_sum, total, errs,
-    load_sem, across_send, across_recv, along_send, along_recv,
+    load_sem, heard, across_send, across_recv, along_send, along_recv,
     pop_send, pop_recv, known_send, known_recv, near_send, near_recv, far_send, far_recv, err_send, err_recv,
 ):
     me = lax.axis_index("pop")
@@ -96,11 +96,26 @@
     beside = me + 1 - 2 * side
     aligned = [2 * lax.rem(level + i, levels) + side for i in range(1, levels)]
     near_mp, far_mp = mc + 1 - 2 * lax.rem(mc, 2), lax.rem(mc + 2, n_mp)
-    partners = [(p, mc) for p in aligned[::-1] + [beside]] + [(me, near_mp), (me, far_mp)]
+    partners = [(beside, mc), (me, near_mp), (me, far_mp)]
+
+    def tell(semaphore, p, m=mc):
+        pl.semaphore_signal(
+            semaphore, inc=1, device_id={"pop": p, "mp": m}, device_id_type=MESH
+        )
+
+    def tell_neighbours(semaphore):
+        @pl.when(level > 0)
+        def _():
+            tell(semaphore, me - 2)
+
+        @pl.when(level < levels - 1)
+        def _():
+            tell(semaphore, me + 2)
+
+    neighbours = jnp.where(level > 0, 1, 0) + jnp.where(level < levels - 1, 1, 0)
+    tell_neighbours(barrier)
     for p, m in partners:
-        pl.semaphore_signal(
-            barrier, inc=1, device_id={"pop": p, "mp": m}, device_id_type=MESH
-        )
+        tell(barrier, p, m)
 
     if lead:
         wq_ref[pl.ds(pl.multiple_of(jnp.where(odd, 0, cols), 16), lead), :] = jnp.zeros(
@@ -117,7 +132,8 @@
         part[b % 2, b // 2] = base[b * own_tok:(b + 1) * own_tok].astype(LINK)
     mine_q[...] = (qr_ref[...].astype(f32) * factor).astype(bf16)
 
-    pl.semaphore_wait(barrier, len(partners))
+    pl.semaphore_wait(barrier, len(partners) + neighbours)
+    tell_neighbours(heard.at[0])
 
     ways = [
         sorted(range(levels), key=lambda t: (-abs(t - u), (t < levels // 2) == (u < levels // 2)))
@@ -188,7 +204,6 @@
 
     for g in range(2):
         across(0, g).start()
-    give(0, aligned)
     for k in range(1, levels):
         for g in range(2):
             across(k, g).start()
@@ -196,14 +211,14 @@
         load.wait()
     ql = ql_ref[...]
     mine_l[...] = dot(ql, tok_ref[...], ((1,), (1,))).astype(bf16)
-    give(1, aligned)
+    for r in range(1, levels - 2):
+        pl.semaphore_wait(heard.at[r - 1], neighbours)
+        tell_neighbours(heard.at[r])
     mine_o[...] = ol_ref[...]
     scaled = (or_ref[...].astype(f32) * factor).astype(bf16)
     for q in range(n_pop):
         mine_a[q] = ql[:, q * cols:(q + 1) * cols]
         mine_b[q] = scaled[:, q * cols:(q + 1) * cols]
-    give(2, aligned)
-    give(3, aligned)
     packs_b[me] = mine_b[me]
     packs_a[me] = mine_a[me]
     packs_l[me] = mine_l[...]
@@ -217,7 +232,12 @@
     key = (key * cos_ref[...] + pltpu.roll(key, HEAD_DIM // 2, 1) * sin_ref[...]).astype(bf16)
     values[:HEAD_DIM] = pair[:, HEAD_DIM:].T.astype(bf16)
     values[HEAD_DIM:] = jnp.ones((values.shape[0] - HEAD_DIM, tok), bf16)
+    pl.semaphore_wait(heard.at[levels - 3], neighbours)
+    tell(heard.at[levels - 2], beside)
+    for kind in range(4):
+        give(kind, aligned)
     relay(0)
+    pl.semaphore_wait(heard.at[levels - 2], 1)
     give(0, crossed)
     give(1, crossed)
     spot = lax.broadcasted_iota(jnp.int32, (tok, HEAD_DIM), 0)
@@ -554,7 +574,7 @@
             pltpu.VMEM((n_pop, cols // n_mp, rows), f32),
             pltpu.VMEM((8, rows), f32),
             pltpu.VMEM((n_dev, 1, 128), f32),
-            dma((16,)),
+            dma((16,)), pltpu.SemaphoreType.REGULAR((n_pop // 2 - 1,)),
             dma, dma((n_pop // 2, 2)), dma, dma,
             dma((5,)), dma((5,)), dma, dma((n_pop,)),
             dma, dma((n_pop,)), dma, dma((n_pop,)),

time: 45.5 us -> 45.8 us (level)
  no operation moved by 1% of the time
where the time goes in v4:
time: 45.8 us; the launch traced here: 45.6 us
  Pallas kernels  44.3 us (97%)
  between operations  1.29 us (3%)
    pallas_call x1, Pallas kernels, per_device_fast(): pl.pallas_call(functools.partial(forward_kernel, n_pop, n_mp, width), nam...  42.2 us
    pallas_call x1, Pallas kernels, per_device_fast(): pl.pallas_call(grad_kernel, name='grads', out_shape=(grad, grad, jax.Shap...  2.06 us

profile of v4, /device:TPU:0, one launch (start us, length us, event | category | flops | bytes accessed | tf_op | source)
XLA Modules:
  0.0 45.6 jit_solution(7921374784726255558)
XLA Ops:
  1.3 42.2 %forward.1 = (bf16[2,32,896]{2,1,0:T(8,128)(2,1)S(1)}, bf16[2,512,128]{2,1,0:T(8,128)(2,1)S(1)}, f32[8,128]{1,0:T(8,128)S(1)}) custom-call(bf16[256,3584]{1,0:T(8,128)(2,1)} %tok_hbm.1, bf16[448,896]{1,0:T(8,128)(2,1)} %wq_hbm.1, bf16[3584,128]{1,0:T(8,128)(2,1)} %wk_hbm.1, bf16[3584,128]{1,0:T(8,128)(2,1)} %wv_hbm.1, bf16[448,896]{1,0:T(8,128)(2,1)} %bitcast.10, ...), custom_call_target="tpu_custom_call" | custom-call | tf_op jit(solution)/shard_map/forward/pallas_call | solution.py:526
  43.5 2.1 %grads.1 = (f32[448,896]{1,0:T(8,128)}, f32[448,896]{1,0:T(8,128)}, f32[1]{0:T(128)}) custom-call(bf16[2,32,896]{2,1,0:T(8,128)(2,1)S(1)} %get-tuple-element.9.rows_ref, bf16[2,512,128]{2,1,0:T(8,128)(2,1)S(1)} %get-tuple-element.10.left_ref, f32[8,128]{1,0:T(8,128)S(1)} %get-tuple-element.11.stat_ref), custom_call_target="tpu_custom_call" | custom-call | tf_op jit(solution)/shard_map/grads/pallas_call | solution.py:591
